TPU v7x, 32 devices: a whole 2x2x4 slice. The times are simulated.
32 devices in a mesh: chain: 4 (over x, core), quad: 8 (over z, y).
Axes of the slice: x: 2, y: 2, z: 4, core: 2. Of those that a mesh axis runs over, the one named last changes fastest.
Arguments:
- sections: bfloat16 [4, 4096, 4096], P('chain', 'quad'), may hold values from -8 to 8
- anchor: bfloat16 [4096, 4096], P('quad'), may hold values from -8 to 8
Outputs:
- registered: bfloat16 [4, 4096, 4096], P('chain', 'quad')
- accumulated: float32 [4, 64, 128], P('chain')
All inputs are finite; a program needn't handle non-finite values.
Results may differ from a plain program's by a relative error of at most 0.00135.
The roundings to bfloat16 on the way count: a program that leaves them out, or rounds other values in their place, can miss the bound.
Values may be sent and summed in bfloat16 or wider, within the bound.
A program may use at most 128 MiB of HBM per device.

v0:
```python
import functools

import jax
import jax.numpy as jnp
from jax import lax
from jax.experimental import pallas as pl
from jax.experimental.pallas import tpu as pltpu
from jax.sharding import PartitionSpec as P

GRID_SIZE = 64
ITERATIONS = 4
EPSILON = 1e-06
SMOOTHING = 0.25
EXACT = lax.Precision.HIGHEST
BAND = 4
SPLIT = 4
LANES = 128
EDGE = 8
BLOCK_ROWS = 32
BLOCK_COLS = 512
VMEM_BYTES = 60 * 2**20


def with_ends(array, axis, dim):
    size, length = lax.axis_size(axis), array.shape[dim]
    up = [(i, i + 1) for i in range(size - 1)]
    down = [(j, i) for i, j in up]
    before = lax.ppermute(lax.slice_in_dim(array, length - 1, length, axis=dim), axis, up)
    after = lax.ppermute(lax.slice_in_dim(array, 0, 1, axis=dim), axis, down)
    return before, after


def spline_weight(offset):
    distance = jnp.abs(offset)
    near_part = 2.0 / 3.0 - distance * distance + 0.5 * distance * distance * distance
    remain = 2.0 - distance
    far_part = remain * remain * remain / 6.0
    return jnp.where(distance < 1.0, near_part, jnp.where(distance < 2.0, far_part, 0.0))


def spline_basis(first_row, pixel_count, extent):
    spacing = extent // GRID_SIZE
    pixels = (first_row + jnp.arange(pixel_count, dtype=jnp.int32)).astype(jnp.float32)
    knot_pos = jnp.arange(GRID_SIZE, dtype=jnp.int32).astype(jnp.float32)
    offset = (pixels[:, None] + 0.5) / spacing - knot_pos[None, :] - 0.5
    return spline_weight(offset)


def fill_wide(m_ref, edges_ref, wide):
    rows, cols = m_ref.shape
    height = rows + 2 * EDGE
    zeros = jnp.zeros((height, LANES), jnp.float32)
    wide[:, pl.ds(0, LANES)] = zeros
    wide[:, pl.ds(cols + LANES, LANES)] = zeros
    wide[pl.ds(0, EDGE), pl.ds(LANES, cols)] = edges_ref[pl.ds(0, EDGE), :]
    wide[pl.ds(EDGE + rows, EDGE), pl.ds(LANES, cols)] = edges_ref[pl.ds(EDGE, EDGE), :]

    @pl.loop(0, rows // BLOCK_ROWS)
    def _(i):
        r = pl.multiple_of(i * BLOCK_ROWS, BLOCK_ROWS)
        wide[pl.ds(EDGE + r, BLOCK_ROWS), pl.ds(LANES, cols)] = m_ref[
            pl.ds(r, BLOCK_ROWS), :
        ].astype(jnp.float32)


def slopes_of(wide, r, c):
    across = wide[pl.ds(r + EDGE, BLOCK_ROWS), pl.ds(c, BLOCK_COLS + 2 * LANES)]
    total = BLOCK_COLS + 2 * LANES
    slope_x = 0.5 * (pltpu.roll(across, total - 1, 1) - pltpu.roll(across, 1, 1))
    slope_x = slope_x[:, LANES : LANES + BLOCK_COLS]
    value = across[:, LANES : LANES + BLOCK_COLS]
    down = wide[pl.ds(r, BLOCK_ROWS + 2 * EDGE), pl.ds(c + LANES, BLOCK_COLS)]
    tall = BLOCK_ROWS + 2 * EDGE
    slope_y = 0.5 * (pltpu.roll(down, tall - 1, 0) - pltpu.roll(down, 1, 0))
    slope_y = slope_y[EDGE : EDGE + BLOCK_ROWS, :]
    return value, slope_x, slope_y


def fold(array):
    rows, cols = array.shape
    out = jnp.zeros((8, LANES), jnp.float32)
    for a in range(rows // 8):
        for b in range(cols // LANES):
            out = out + array[a * 8 : a * 8 + 8, b * LANES : b * LANES + LANES]
    return out


def tables_kernel(m_ref, f_ref, edges_ref, basis_ref, pairs_ref, lin_ref, quad_ref, sums_ref, wide, fields):
    rows, cols = m_ref.shape
    span = fields.shape[2]
    fill_wide(m_ref, edges_ref, wide)
    sums_ref[...] = jnp.zeros_like(sums_ref)
    lin_ref[...] = jnp.zeros_like(lin_ref)
    quad_ref[...] = jnp.zeros_like(quad_ref)
    per_row = span // BLOCK_COLS

    @pl.loop(0, cols // span)
    def _(part):
        start = pl.multiple_of(part * span, span)

        @pl.loop(0, rows // BLOCK_ROWS * per_row)
        def _(step):
            i, j = step // per_row, step % per_row
            r = pl.multiple_of(i * BLOCK_ROWS, BLOCK_ROWS)
            c = pl.multiple_of(j * BLOCK_COLS, BLOCK_COLS)
            at = pl.multiple_of(start + c, BLOCK_COLS)
            value, sx, sy = slopes_of(wide, r, at)
            fixed = f_ref[pl.ds(r, BLOCK_ROWS), pl.ds(at, BLOCK_COLS)].astype(jnp.float32)
            rest = fixed - value
            here = (pl.ds(r, BLOCK_ROWS), pl.ds(c, BLOCK_COLS))
            for k, field in enumerate((rest * sx, rest * sy, value * sx, value * sy)):
                high = field.astype(jnp.bfloat16)
                fields[(k, *here)] = high
                fields[(SPLIT + k, *here)] = (field - high.astype(jnp.float32)).astype(jnp.bfloat16)
            for k, field in enumerate((sx, sy, sx * sx, sx * sy, sy * sy)):
                fields[(2 * SPLIT + k, *here)] = field.astype(jnp.bfloat16)
            for k, field in enumerate((fixed, value, rest * value, value * value)):
                sums_ref[k] += fold(field)

        basis = basis_ref[pl.ds(start, span), :]
        dot = functools.partial(jnp.dot, preferred_element_type=jnp.float32)
        for k in range(3):
            x, y = ((0, 1), (2, 3), (2 * SPLIT, 2 * SPLIT + 1))[k]
            along_x, along_y = dot(fields[x], basis), dot(fields[y], basis)
            if k < 2:
                along_x += dot(fields[SPLIT + x], basis)
                along_y += dot(fields[SPLIT + y], basis)
            lin_ref[k] += jnp.concatenate([along_x[:, :GRID_SIZE], along_y[:, :GRID_SIZE]], axis=1)
        pairs = pairs_ref[0, pl.ds(start, span), :]
        small = pairs_ref[1, pl.ds(start, span), :]
        xx, xy, yy = (
            dot(fields[2 * SPLIT + 2 + k], pairs) + dot(fields[2 * SPLIT + 2 + k], small) for k in range(3)
        )
        for d in range(BAND):
            at = slice(d * GRID_SIZE, (d + 1) * GRID_SIZE)
            quad_ref[d] += jnp.concatenate([xx[:, at], yy[:, at]], axis=1)
            quad_ref[BAND + d] += jnp.concatenate([xy[:, at], xy[:, at]], axis=1)


def tables(moving, fixed, edges, basis, pairs):
    rows, cols = moving.shape
    span = cols // 4
    vmem = pl.BlockSpec(memory_space=pltpu.VMEM)
    return pl.pallas_call(
        tables_kernel,
        out_shape=(
            jax.ShapeDtypeStruct((3, rows, 2 * GRID_SIZE), jnp.float32),
            jax.ShapeDtypeStruct((2 * BAND, rows, 2 * GRID_SIZE), jnp.float32),
            jax.ShapeDtypeStruct((4, 8, LANES), jnp.float32),
        ),
        in_specs=[vmem] * 5,
        out_specs=[vmem] * 3,
        scratch_shapes=[
            pltpu.VMEM((rows + 2 * EDGE, cols + 2 * LANES), jnp.float32),
            pltpu.VMEM((2 * SPLIT + 5, rows, span), jnp.bfloat16),
        ],
        compiler_params=pltpu.CompilerParams(vmem_limit_bytes=VMEM_BYTES),
    )(moving, fixed, edges, basis, pairs)


def warp_kernel(m_ref, edges_ref, mixed_ref, flat_ref, out_ref, wide, stage_x, stage_y):
    rows, cols = m_ref.shape
    fill_wide(m_ref, edges_ref, wide)
    span = stage_x.shape[1]

    @pl.loop(0, cols // span)
    def _(chunk):
        start = pl.multiple_of(chunk * span, span)
        flat = flat_ref[:, pl.ds(start, span)]
        stage_x[...] = jnp.dot(mixed_ref[:, :GRID_SIZE], flat, preferred_element_type=jnp.float32)
        stage_y[...] = jnp.dot(mixed_ref[:, GRID_SIZE:], flat, preferred_element_type=jnp.float32)
        per_row = span // BLOCK_COLS

        @pl.loop(0, rows // BLOCK_ROWS * per_row)
        def _(step):
            i, j = step // per_row, step % per_row
            r = pl.multiple_of(i * BLOCK_ROWS, BLOCK_ROWS)
            c = pl.multiple_of(j * BLOCK_COLS, BLOCK_COLS)
            value, sx, sy = slopes_of(wide, r, pl.multiple_of(start + c, BLOCK_COLS))
            here = (pl.ds(r, BLOCK_ROWS), pl.ds(c, BLOCK_COLS))
            out = value + stage_x[here] * sx + stage_y[here] * sy
            out_ref[pl.ds(r, BLOCK_ROWS), pl.ds(pl.multiple_of(start + c, BLOCK_COLS), BLOCK_COLS)] = (
                out.astype(jnp.bfloat16)
            )


def warp(moving, edges, mixed, flat):
    rows, cols = moving.shape
    vmem = pl.BlockSpec(memory_space=pltpu.VMEM)
    return pl.pallas_call(
        warp_kernel,
        out_shape=jax.ShapeDtypeStruct((rows, cols), jnp.bfloat16),
        in_specs=[vmem] * 4,
        out_specs=vmem,
        scratch_shapes=[
            pltpu.VMEM((rows + 2 * EDGE, cols + 2 * LANES), jnp.float32),
            pltpu.VMEM((rows, 1024), jnp.float32),
            pltpu.VMEM((rows, 1024), jnp.float32),
        ],
        compiler_params=pltpu.CompilerParams(vmem_limit_bytes=VMEM_BYTES),
    )(moving, edges, mixed, flat)


def local(sections, anchor):
    _, rows, columns = sections.shape
    moving = sections[0]
    chain = lax.axis_size("chain")
    height = rows * lax.axis_size("quad")
    pixel_count = height * columns
    row_basis = spline_basis(lax.axis_index("quad") * rows, rows, height)
    basis = spline_basis(0, columns, columns).astype(jnp.bfloat16)
    wide_basis = basis.astype(jnp.float32)
    pairs = jnp.concatenate(
        [
            wide_basis * jnp.pad(wide_basis[:, d:], ((0, 0), (0, d)))
            for d in range(BAND)
        ],
        axis=1,
    )
    large = lax.reduce_precision(pairs, 8, 7)
    pairs = jnp.stack([large, pairs - large]).astype(jnp.bfloat16)
    prior = lax.ppermute(moving, "chain", [(i, i + 1) for i in range(chain - 1)])
    fixed = jnp.where(lax.axis_index("chain") == 0, anchor, prior)
    before, after = with_ends(moving, "quad", 0)
    edges = jnp.concatenate(
        [
            jnp.broadcast_to(before, (EDGE, columns)),
            jnp.broadcast_to(after, (EDGE, columns)),
        ],
        axis=0,
    ).astype(jnp.float32)
    padded_basis = jnp.pad(basis, ((0, 0), (0, LANES - GRID_SIZE)))
    lin, quad, sums = tables(moving, fixed, edges, padded_basis, pairs)
    gather = functools.partial(jnp.einsum, "hg,hk->gk", row_basis, precision=EXACT)
    totals = jnp.sum(sums, axis=(1, 2))
    grad_rest, grad_still, grad_ones, totals = lax.psum(
        (gather(lin[0]), gather(lin[1]), gather(lin[2]), totals), "quad"
    )
    fixed_mean = totals[0] / pixel_count
    rest_total = totals[2]
    coefficients = jnp.zeros((GRID_SIZE, 2 * GRID_SIZE), jnp.float32)
    for iteration in range(ITERATIONS):
        moving_sum, moving_sq, cross_sum = totals[1], totals[3], rest_total + totals[3]
        grad_extra = jnp.zeros_like(coefficients)
        smooth = jnp.zeros_like(coefficients)
        if iteration:
            mixed = jnp.einsum("hg,gk->hk", row_basis, coefficients, precision=EXACT)
            mixed = lax.reduce_precision(mixed, 8, 7)
            other = jnp.roll(mixed, GRID_SIZE, 1)
            moved = jnp.zeros_like(mixed)
            for d in range(BAND):
                moved += quad[d] * jnp.roll(mixed, -d, 1) + quad[BAND + d] * jnp.roll(other, -d, 1)
                if d:
                    moved += jnp.roll(quad[d] * mixed + quad[BAND + d] * other, d, 1)
            scalars = jnp.stack(
                [
                    jnp.sum(mixed * lin[2]),
                    jnp.sum(mixed * (2.0 * lin[1] + moved)),
                    jnp.sum(mixed * (lin[0] + lin[1])),
                ]
            )
            grad_extra, scalars = lax.psum((gather(moved), scalars), "quad")
            moving_sum += scalars[0]
            moving_sq += scalars[1]
            cross_sum += scalars[2]
            before, after = with_ends(coefficients[None], "chain", 0)
            smooth = before[0] - 2.0 * coefficients + after[0]
        moving_mean = moving_sum / pixel_count
        moving_var = moving_sq - pixel_count * moving_mean * moving_mean
        cross_var = cross_sum - pixel_count * fixed_mean * moving_mean
        denominator = jnp.sqrt(moving_var + EPSILON)
        ratio = cross_var / denominator / (moving_var + EPSILON)
        gradient = pixel_count * (
            (grad_rest + grad_still - fixed_mean * grad_ones) / denominator
            - ratio * (grad_still + grad_extra - moving_mean * grad_ones)
        )
        direction = gradient / jnp.sqrt(jnp.mean(gradient * gradient) + EPSILON)
        coefficients = coefficients + direction / ITERATIONS + SMOOTHING * smooth
    everyone = lax.all_gather(coefficients, "chain")
    mine = jnp.arange(chain) <= lax.axis_index("chain")
    accumulated = jnp.sum(jnp.where(mine[:, None, None], everyone, 0.0), axis=0)
    mixed = jnp.einsum("hg,gk->hk", row_basis, accumulated, precision=EXACT).astype(jnp.bfloat16)
    registered = warp(moving, edges, mixed, basis.T)
    return registered[None], accumulated[None]


def solution(mesh):
    in_specs = (P("chain", "quad", None), P("quad", None))
    out_specs = (P("chain", "quad", None), P("chain", None, None))
    return jax.shard_map(local, mesh=mesh, in_specs=in_specs, out_specs=out_specs, check_vma=False)
```

profile of v0, /device:TPU:0, one launch (start us, length us, event | category | flops | bytes accessed | tf_op | source)
XLA Modules:
  0.0 393.4 jit_solution(17484194050106082476)
XLA Ops:
  7.2 4.3 %collective-permute-start.2 = (bf16[512,4096]{1,0:T(8,128)(2,1)}, bf16[512,4096]{1,0:T(8,128)(2,1)}, u32[]{:S(2)}, u32[]{:S(2)}) collective-permute-start(bf16[512,4096]{1,0:T(8,128)(2,1)} %bitcast.254), channel_id=1, source_target_pairs={{0,8},{8,16},{16,24},{1,9},{9,17},{17,25},{2,10},{10,18},{18,26},{... | collective-permute-start | bytes 12582920 | tf_op jit(solution)/shard_map/ppermute | solution.py:222
  12.4 4.2 %collective-permute-start = (bf16[1,4096]{1,0:T(2,128)(2,1)S(1)}, bf16[1,4096]{1,0:T(2,128)(2,1)S(1)}, u32[]{:S(2)}, u32[]{:S(2)}) collective-permute-start(bf16[1,4096]{1,0:T(2,128)(2,1)S(1)} %get-tuple-element.46), channel_id=1, source_target_pairs={{0,1},{1,2},{2,3},{3,4},{4,5},{5,6},{6,7},{8,9},{9,10},{10,11},{11... | collective-permute-start | bytes 24584 | tf_op jit(solution)/shard_map/ppermute | solution.py:28
  18.0 2.4 multiply_bitcast_fusion.3
  20.4 1.9 slice.452
  22.4 2.0 slice.453
  24.4 2.0 slice.454
  26.3 3.8 multiply_bitcast_fusion.2
  30.2 2.1 reduce-precision_convert_fusion
  32.3 2.3 pad_maximum_fusion.1.pairs_ref
  34.6 1.5 fusion.11.flat_ref
  38.3 4.6 %broadcast_select_fusion.f_ref = bf16[512,4096]{1,0:T(8,128)(2,1)} fusion(bf16[512,4096]{1,0:T(8,128)(2,1)} %param.3, bf16[512,4096]{1,0:T(8,128)(2,1)} %collective-permute-done.2, pred[]{:T(512)S(6)} %eq.3), kind=kLoop, calls=%fused_computation.5 | loop fusion | flops 2097152 | bytes 12582913 | tf_op jit(solution)/shard_map/jit(_where)/select_n | solution.py:223
  42.9 45.4 %shard_map.41 = (f32[3,512,128]{2,1,0:T(8,128)}, f32[8,512,128]{2,1,0:T(8,128)}, f32[4,8,128]{2,1,0:T(8,128)}) custom-call(bf16[512,4096]{1,0:T(8,128)(2,1)} %bitcast.255, bf16[512,4096]{1,0:T(8,128)(2,1)} %broadcast_select_fusion.f_ref, f32[16,4096]{1,0:T(8,128)} %maximum_convert_fusion.edges_ref, bf16[4096,128]{1,0:T(8,128)(2,1)} %pad.16.basis_ref, ...), custom_call_target="tpu_custom_call" | custom-call | tf_op jit(solution)/shard_map/pallas_call | solution.py:144
  88.3 2.4 fusion.61
  90.7 2.3 fusion.68
  93.0 1.4 fusion.66
  95.0 92.3 %all-reduce.10.cloned.1.call-done = (f32[64,128]{1,0:T(8,128)}, f32[64,128]{1,0:T(8,128)}, f32[64,128]{1,0:T(8,128)}, f32[4]{0:T(128)}) async-done(((f32[64,128]{1,0:T(8,128)}, f32[64,128]{1,0:T(8,128)}, f32[64,128]{1,0:T(8,128)}, f32[4]{0:T(128)}), (f32[64,128]{1,0:T(8,128)}, f32[64,128]{1,0:T(8,128)}, f32[64,128]{1,0:T(8,128)}, f32[4]{0:T(128)})) %all-reduce.10.cloned.1.call-update) | async-done | bytes 98336 | tf_op jit(solution)/shard_map/psum | solution.py:236
  187.3 1.5 fusion.186
  193.3 1.4 multiply_reduce_fusion.9
  199.1 1.3 fusion.63
  201.1 2.0 pad_maximum_fusion.5
  203.1 36.5 %all-reduce.6 = (f32[64,128]{1,0:T(8,128)S(1)}, f32[3]{0:T(128)S(1)}) all-reduce(f32[64,128]{1,0:T(8,128)S(1)} %fusion.83, f32[3]{0:T(128)S(1)} %pad_maximum_fusion.5), channel_id=1, replica_groups=mesh['chain'=4,'quad'=8] {'quad'}, use_global_device_ids=true, to_apply=%region_10.11 | all-reduce | flops 8195 | bytes 65560 | tf_op jit(solution)/shard_map/psum | solution.py:262
  251.0 1.3 fusion.64
  253.1 2.0 pad_maximum_fusion.6
  255.0 33.4 %all-reduce.5 = (f32[64,128]{1,0:T(8,128)S(1)}, f32[3]{0:T(128)S(1)}) all-reduce(f32[64,128]{1,0:T(8,128)S(1)} %fusion.80, f32[3]{0:T(128)S(1)} %pad_maximum_fusion.6), channel_id=1, replica_groups=mesh['chain'=4,'quad'=8] {'quad'}, use_global_device_ids=true, to_apply=%region_16.17 | all-reduce | flops 8195 | bytes 65560 | tf_op jit(solution)/shard_map/psum | solution.py:262
  292.3 1.5 collective-permute-start.6
  297.1 2.8 collective-permute-done.6
  302.7 1.3 fusion.65
  304.7 2.0 pad_maximum_fusion.7
  306.7 35.2 %all-reduce.4 = (f32[64,128]{1,0:T(8,128)S(1)}, f32[3]{0:T(128)S(1)}) all-reduce(f32[64,128]{1,0:T(8,128)S(1)} %fusion.77, f32[3]{0:T(128)S(1)} %pad_maximum_fusion.7), channel_id=1, replica_groups=mesh['chain'=4,'quad'=8] {'quad'}, use_global_device_ids=true, to_apply=%region_22.23 | all-reduce | flops 8195 | bytes 65560 | tf_op jit(solution)/shard_map/psum | solution.py:262
  350.3 3.2 collective-permute-done.8
  353.6 7.8 %all-gather = f32[256,128]{1,0:T(8,128)S(1)} all-gather(f32[64,128]{1,0:T(8,128)S(1)} %fusion.90), channel_id=2, replica_groups=mesh['chain'=4,'quad'=8] {'chain'}, dimensions={0}, use_global_device_ids=true | all-gather | bytes 163840 | tf_op jit(solution)/shard_map/all_gather | solution.py:279
  362.6 23.9 %shard_map.42 = bf16[512,4096]{1,0:T(8,128)(2,1)} custom-call(bf16[512,4096]{1,0:T(8,128)(2,1)} %bitcast.256, f32[16,4096]{1,0:T(8,128)} %maximum_convert_fusion.edges_ref, bf16[512,128]{1,0:T(8,128)(2,1)} %convolution_convert_fusion.mixed_ref, bf16[64,4096]{1,0:T(8,128)(2,1)} %fusion.11.flat_ref), custom_call_target="tpu_custom_call" | custom-call | tf_op jit(solution)/shard_map/pallas_call | solution.py:190
  (106 shorter events, 27.9 us)
Async XLA Ops:
  7.2 180.1 %all-reduce.10.cloned.1.call-start = ((), (), s32[]{:S(2)}) async-start(), calls=%async_computation | async-start | bytes 197632 | tf_op jit(solution)/shard_map/psum | solution.py:236
  7.2 31.0 %collective-permute-start.2 = (bf16[512,4096]{1,0:T(8,128)(2,1)}, bf16[512,4096]{1,0:T(8,128)(2,1)}, u32[]{:S(2)}, u32[]{:S(2)}) collective-permute-start(bf16[512,4096]{1,0:T(8,128)(2,1)} %bitcast.254), channel_id=1, source_target_pairs={{0,8},{8,16},{16,24},{1,9},{9,17},{17,25},{2,10},{10,18},{18,26},{... | collective-permute-start | bytes 12582920 | tf_op jit(solution)/shard_map/ppermute | solution.py:222
  12.4 24.9 %collective-permute-start = (bf16[1,4096]{1,0:T(2,128)(2,1)S(1)}, bf16[1,4096]{1,0:T(2,128)(2,1)S(1)}, u32[]{:S(2)}, u32[]{:S(2)}) collective-permute-start(bf16[1,4096]{1,0:T(2,128)(2,1)S(1)} %get-tuple-element.46), channel_id=1, source_target_pairs={{0,1},{1,2},{2,3},{3,4},{4,5},{5,6},{6,7},{8,9},{9,10},{10,11},{11... | collective-permute-start | bytes 24584 | tf_op jit(solution)/shard_map/ppermute | solution.py:28
  16.7 20.7 %collective-permute-start.1 = (bf16[1,4096]{1,0:T(2,128)(2,1)S(1)}, bf16[1,4096]{1,0:T(2,128)(2,1)S(1)}, u32[]{:S(2)}, u32[]{:S(2)}) collective-permute-start(bf16[1,4096]{1,0:T(2,128)(2,1)S(1)} %get-tuple-element.47), channel_id=1, source_target_pairs={{1,0},{2,1},{3,2},{4,3},{5,4},{6,5},{7,6},{9,8},{10,9},{11,10},{12... | collective-permute-start | bytes 24584 | tf_op jit(solution)/shard_map/ppermute | solution.py:29
  26.3 3.8 copy-start.1
  88.3 4.7 %copy-start.2 = (f32[3,512,128]{2,1,0:T(8,128)S(1)}, f32[3,512,128]{2,1,0:T(8,128)}, u32[]{:S(2)}) copy-start(f32[3,512,128]{2,1,0:T(8,128)} %get-tuple-element.5) | copy-start | bytes 2359300
  88.3 6.0 %copy-start.7 = (f32[4,8,128]{2,1,0:T(8,128)S(1)}, f32[4,8,128]{2,1,0:T(8,128)}, u32[]{:S(2)}) copy-start(f32[4,8,128]{2,1,0:T(8,128)} %get-tuple-element.6) | copy-start | bytes 49156
  196.8 1.6 copy-start
  199.0 47.7 %copy-start.3 = (f32[64,128]{1,0:T(8,128)S(1)}, f32[64,128]{1,0:T(8,128)}, u32[]{:S(2)}) copy-start(f32[64,128]{1,0:T(8,128)} %get-tuple-element.23) | copy-start | bytes 98308
  199.0 47.7 %copy-start.4 = (f32[64,128]{1,0:T(8,128)S(1)}, f32[64,128]{1,0:T(8,128)}, u32[]{:S(2)}) copy-start(f32[64,128]{1,0:T(8,128)} %get-tuple-element.24) | copy-start | bytes 98308
  199.1 47.7 %copy-start.5 = (f32[64,128]{1,0:T(8,128)S(1)}, f32[64,128]{1,0:T(8,128)}, u32[]{:S(2)}) copy-start(f32[64,128]{1,0:T(8,128)} %get-tuple-element.25) | copy-start | bytes 98308
  242.1 5.9 %collective-permute-start.3 = (f32[1,64,128]{2,1,0:T(8,128)S(1)}, f32[1,64,128]{2,1,0:T(8,128)S(1)}, u32[]{:S(2)}, u32[]{:S(2)}) collective-permute-start(f32[1,64,128]{2,1,0:T(8,128)S(1)} %multiply_bitcast_fusion.4), channel_id=1, source_target_pairs={{0,8},{8,16},{16,24},{1,9},{9,17},{17,25},{2,10},{10,18},{18,26},{... | collective-permute-start | bytes 98312 | tf_op jit(solution)/shard_map/ppermute | solution.py:28
  243.4 4.8 %collective-permute-start.4 = (f32[1,64,128]{2,1,0:T(8,128)S(1)}, f32[1,64,128]{2,1,0:T(8,128)S(1)}, u32[]{:S(2)}, u32[]{:S(2)}) collective-permute-start(f32[1,64,128]{2,1,0:T(8,128)S(1)} %multiply_bitcast_fusion.4), channel_id=1, source_target_pairs={{8,0},{16,8},{24,16},{9,1},{17,9},{25,17},{10,2},{18,10},{26,18},{... | collective-permute-start | bytes 98312 | tf_op jit(solution)/shard_map/ppermute | solution.py:29
  291.0 6.1 %collective-permute-start.5 = (f32[1,64,128]{2,1,0:T(8,128)S(1)}, f32[1,64,128]{2,1,0:T(8,128)S(1)}, u32[]{:S(2)}, u32[]{:S(2)}) collective-permute-start(f32[1,64,128]{2,1,0:T(8,128)S(1)} %bitcast.270), channel_id=1, source_target_pairs={{0,8},{8,16},{16,24},{1,9},{9,17},{17,25},{2,10},{10,18},{18,26},{... | collective-permute-start | bytes 98312 | tf_op jit(solution)/shard_map/ppermute | solution.py:28
  292.3 7.6 %collective-permute-start.6 = (f32[1,64,128]{2,1,0:T(8,128)S(1)}, f32[1,64,128]{2,1,0:T(8,128)S(1)}, u32[]{:S(2)}, u32[]{:S(2)}) collective-permute-start(f32[1,64,128]{2,1,0:T(8,128)S(1)} %bitcast.271), channel_id=1, source_target_pairs={{8,0},{16,8},{24,16},{9,1},{17,9},{25,17},{10,2},{18,10},{26,18},{... | collective-permute-start | bytes 98312 | tf_op jit(solution)/shard_map/ppermute | solution.py:29
  344.4 5.9 %collective-permute-start.7 = (f32[1,64,128]{2,1,0:T(8,128)S(1)}, f32[1,64,128]{2,1,0:T(8,128)S(1)}, u32[]{:S(2)}, u32[]{:S(2)}) collective-permute-start(f32[1,64,128]{2,1,0:T(8,128)S(1)} %bitcast.268), channel_id=1, source_target_pairs={{0,8},{8,16},{16,24},{1,9},{9,17},{17,25},{2,10},{10,18},{18,26},{... | collective-permute-start | bytes 98312 | tf_op jit(solution)/shard_map/ppermute | solution.py:28
  345.7 7.8 %collective-permute-start.8 = (f32[1,64,128]{2,1,0:T(8,128)S(1)}, f32[1,64,128]{2,1,0:T(8,128)S(1)}, u32[]{:S(2)}, u32[]{:S(2)}) collective-permute-start(f32[1,64,128]{2,1,0:T(8,128)S(1)} %bitcast.269), channel_id=1, source_target_pairs={{8,0},{16,8},{24,16},{9,1},{17,9},{25,17},{10,2},{18,10},{26,18},{... | collective-permute-start | bytes 98312 | tf_op jit(solution)/shard_map/ppermute | solution.py:29
  361.5 25.1 %copy-start.6 = (f32[64,128]{1,0:T(8,128)}, f32[64,128]{1,0:T(8,128)S(1)}, u32[]{:S(2)}) copy-start(f32[64,128]{1,0:T(8,128)S(1)} %select_reduce_fusion) | copy-start | bytes 98308
Sparse Core Ops, SparseCore 0:
  95.1 92.1 all-reduce.9
where the time goes:
time: 394 us; the launch traced here: 393 us
  blocking collectives  113 us (29%)
  waiting for transfers between devices  98.4 us (25%)
  Pallas kernels  69.3 us (18%)
  other arithmetic  34 us (9%)
  between operations  33.6 us (9%)
  starting transfers between devices  17.9 us (5%)
  local copies, waits for them, and re-layouts  16.4 us (4%)
  matrix products  10.9 us (3%)
    psum x3, blocking collectives, local(): grad_extra, scalars = lax.psum((gather(moved), scalars), 'quad')  105 us
    psum x1, waiting for transfers between devices, local(): lax.psum((gather(lin[0]), gather(lin[1]), gather(lin[2]), totals), 'quad')  92.3 us
    pallas_call x1, Pallas kernels, tables(): pl.pallas_call(tables_kernel, out_shape=(jax.ShapeDtypeStruct((3, rows, 2...  45.4 us
    pallas_call x1, Pallas kernels, warp(): pl.pallas_call(warp_kernel, out_shape=jax.ShapeDtypeStruct((rows, cols),...  23.9 us
    ppermute x4, starting transfers between devices, with_ends(): lax.ppermute(lax.slice_in_dim(array, length - 1, length, axis=dim), axis,...  8.12 us
  transfers between devices with their start and end apart: 10, of which 4 were waited for; matrix products, arithmetic and copies ran while one was open for 6% of the time, Pallas kernels for 0%

commit v1 on v0

v1 whole, which is shorter than its diff:
```python
import functools

import jax
import jax.numpy as jnp
from jax import lax
from jax.experimental import pallas as pl
from jax.experimental.pallas import tpu as pltpu
from jax.sharding import PartitionSpec as P

GRID_SIZE = 64
ITERATIONS = 4
EPSILON = 1e-06
SMOOTHING = 0.25
EXACT = lax.Precision.HIGHEST
BAND = 4
SPLIT = 4
LANES = 128
EDGE = 8
BLOCK_ROWS = 32
BLOCK_COLS = 512
VMEM_BYTES = 60 * 2**20


def spline_weight(offset):
    distance = jnp.abs(offset)
    near_part = 2.0 / 3.0 - distance * distance + 0.5 * distance * distance * distance
    remain = 2.0 - distance
    far_part = remain * remain * remain / 6.0
    return jnp.where(distance < 1.0, near_part, jnp.where(distance < 2.0, far_part, 0.0))


def spline_basis(first_row, pixel_count, extent):
    spacing = extent // GRID_SIZE
    pixels = (first_row + jnp.arange(pixel_count, dtype=jnp.int32)).astype(jnp.float32)
    knot_pos = jnp.arange(GRID_SIZE, dtype=jnp.int32).astype(jnp.float32)
    offset = (pixels[:, None] + 0.5) / spacing - knot_pos[None, :] - 0.5
    return spline_weight(offset)


def with_ends(array, axis, dim):
    size, length = lax.axis_size(axis), array.shape[dim]
    up = [(i, i + 1) for i in range(size - 1)]
    down = [(j, i) for i, j in up]
    before = lax.ppermute(lax.slice_in_dim(array, length - 1, length, axis=dim), axis, up)
    after = lax.ppermute(lax.slice_in_dim(array, 0, 1, axis=dim), axis, down)
    return before, after


def fill_wide(m_ref, edges_ref, wide):
    rows, cols = m_ref.shape
    height = rows + 2 * EDGE
    zeros = jnp.zeros((height, LANES), jnp.float32)
    wide[:, pl.ds(0, LANES)] = zeros
    wide[:, pl.ds(cols + LANES, LANES)] = zeros
    wide[pl.ds(0, EDGE), pl.ds(LANES, cols)] = edges_ref[pl.ds(0, EDGE), :]
    wide[pl.ds(EDGE + rows, EDGE), pl.ds(LANES, cols)] = edges_ref[pl.ds(EDGE, EDGE), :]

    @pl.loop(0, rows // BLOCK_ROWS)
    def _(i):
        r = pl.multiple_of(i * BLOCK_ROWS, BLOCK_ROWS)
        wide[pl.ds(EDGE + r, BLOCK_ROWS), pl.ds(LANES, cols)] = m_ref[
            pl.ds(r, BLOCK_ROWS), :
        ].astype(jnp.float32)


def slopes_of(wide, r, c):
    across = wide[pl.ds(r + EDGE, BLOCK_ROWS), pl.ds(c, BLOCK_COLS + 2 * LANES)]
    total = BLOCK_COLS + 2 * LANES
    slope_x = 0.5 * (pltpu.roll(across, total - 1, 1) - pltpu.roll(across, 1, 1))
    slope_x = slope_x[:, LANES : LANES + BLOCK_COLS]
    value = across[:, LANES : LANES + BLOCK_COLS]
    down = wide[pl.ds(r, BLOCK_ROWS + 2 * EDGE), pl.ds(c + LANES, BLOCK_COLS)]
    tall = BLOCK_ROWS + 2 * EDGE
    slope_y = 0.5 * (pltpu.roll(down, tall - 1, 0) - pltpu.roll(down, 1, 0))
    slope_y = slope_y[EDGE : EDGE + BLOCK_ROWS, :]
    return value, slope_x, slope_y


def fold(array):
    rows, cols = array.shape
    out = jnp.zeros((8, LANES), jnp.float32)
    for a in range(rows // 8):
        for b in range(cols // LANES):
            out = out + array[a * 8 : a * 8 + 8, b * LANES : b * LANES + LANES]
    return out


def warp_kernel(m_ref, edges_ref, mixed_ref, flat_ref, out_ref, wide, stage_x, stage_y):
    rows, cols = m_ref.shape
    fill_wide(m_ref, edges_ref, wide)
    span = stage_x.shape[1]

    @pl.loop(0, cols // span)
    def _(chunk):
        start = pl.multiple_of(chunk * span, span)
        flat = flat_ref[:, pl.ds(start, span)]
        stage_x[...] = jnp.dot(mixed_ref[:, :GRID_SIZE], flat, preferred_element_type=jnp.float32)
        stage_y[...] = jnp.dot(mixed_ref[:, GRID_SIZE:], flat, preferred_element_type=jnp.float32)
        per_row = span // BLOCK_COLS

        @pl.loop(0, rows // BLOCK_ROWS * per_row)
        def _(step):
            i, j = step // per_row, step % per_row
            r = pl.multiple_of(i * BLOCK_ROWS, BLOCK_ROWS)
            c = pl.multiple_of(j * BLOCK_COLS, BLOCK_COLS)
            value, sx, sy = slopes_of(wide, r, pl.multiple_of(start + c, BLOCK_COLS))
            here = (pl.ds(r, BLOCK_ROWS), pl.ds(c, BLOCK_COLS))
            out = value + stage_x[here] * sx + stage_y[here] * sy
            out_ref[pl.ds(r, BLOCK_ROWS), pl.ds(pl.multiple_of(start + c, BLOCK_COLS), BLOCK_COLS)] = (
                out.astype(jnp.bfloat16)
            )


def warp(moving, edges, mixed, flat):
    rows, cols = moving.shape
    vmem = pl.BlockSpec(memory_space=pltpu.VMEM)
    return pl.pallas_call(
        warp_kernel,
        out_shape=jax.ShapeDtypeStruct((rows, cols), jnp.bfloat16),
        in_specs=[vmem] * 4,
        out_specs=vmem,
        scratch_shapes=[
            pltpu.VMEM((rows + 2 * EDGE, cols + 2 * LANES), jnp.float32),
            pltpu.VMEM((rows, 1024), jnp.float32),
            pltpu.VMEM((rows, 1024), jnp.float32),
        ],
        compiler_params=pltpu.CompilerParams(vmem_limit_bytes=VMEM_BYTES),
    )(moving, edges, mixed, flat)


MESH = pl.DeviceIdType.MESH
HEAD = 8
HALO = 16
FIELDS = 7
SPAN = 1024
F32 = jnp.float32
BF16 = jnp.bfloat16


def window_of(knots):
    return 16 + max(8, -(-knots // 8) * 8)


def base_of(strip, knots):
    return lax.div(strip * knots, 8) * 8


def strip_basis(shape, pixel_dim, first_row, first_knot, spacing):
    pixels = (first_row + lax.broadcasted_iota(jnp.int32, shape, pixel_dim)).astype(F32)
    knot_pos = (first_knot + lax.broadcasted_iota(jnp.int32, shape, 1 - pixel_dim)).astype(F32)
    return spline_weight((pixels + 0.5) * (1.0 / spacing) - knot_pos - 0.5)


def column_tables(basis_ref, pairs_ref, spacing):
    middle = GRID_SIZE // 2
    wide = BAND * GRID_SIZE
    shape = (spacing, wide)
    lane = lax.broadcasted_iota(jnp.int32, shape, 1)
    pixel = (middle * spacing + lax.broadcasted_iota(jnp.int32, shape, 0)).astype(F32)
    place = (pixel + 0.5) * (1.0 / spacing) - 0.5
    knot, band = lax.rem(lane, GRID_SIZE), lax.div(lane, GRID_SIZE)
    rounded = lambda values: values.astype(BF16).astype(F32)
    single = rounded(spline_weight(place - knot.astype(F32)))
    product = single * rounded(spline_weight(place - (knot + band).astype(F32)))
    large = rounded(product)
    small = product - large
    one_lane = lax.broadcasted_iota(jnp.int32, (spacing, LANES), 1)
    one_knot = lax.rem(one_lane, GRID_SIZE)

    @pl.loop(0, GRID_SIZE)
    def _(t):
        at = pl.ds(pl.multiple_of(t * spacing, spacing), spacing)
        shift = lax.rem(t - middle + LANES, LANES)
        close = jnp.abs(one_knot - t) <= BAND
        moved = jnp.where(close, pltpu.roll(single[:, :LANES], shift, 1), 0.0)
        for k in range(2):
            half = one_lane < GRID_SIZE if k == 0 else one_lane >= GRID_SIZE
            basis_ref[k, at, :] = jnp.where(half, moved, 0.0).astype(BF16)
        for k in range(wide // LANES):
            cols = slice(k * LANES, (k + 1) * LANES)
            reach = one_knot + (k * LANES // GRID_SIZE + lax.div(one_lane, GRID_SIZE))
            keep = close & (reach < GRID_SIZE)
            for part, values in enumerate((large, small)):
                rolled = jnp.where(keep, pltpu.roll(values[:, cols], shift, 1), 0.0)
                pairs_ref[part, at, cols] = rolled.astype(BF16)


def fill_rows(wide, at, source, row, count, skip=0):
    cols = source.shape[1]
    values = source[pl.ds(row, count + skip), :].astype(F32)
    wide[pl.ds(at, count), pl.ds(LANES, cols)] = values[skip:]


def fill_body(wide, source, offset, rows):
    @pl.loop(0, rows // BLOCK_ROWS)
    def _(i):
        r = pl.multiple_of(i * BLOCK_ROWS, BLOCK_ROWS)
        fill_rows(wide, EDGE + r, source, pl.multiple_of(offset + r, 16), BLOCK_ROWS)


def blocks(rows, start, body):
    per_row = SPAN // BLOCK_COLS

    @pl.loop(0, rows // BLOCK_ROWS * per_row)
    def _(step):
        i, j = lax.div(step, per_row), lax.rem(step, per_row)
        r = pl.multiple_of(i * BLOCK_ROWS, BLOCK_ROWS)
        c = pl.multiple_of(j * BLOCK_COLS, BLOCK_COLS)
        body(r, c, pl.multiple_of(start + c, BLOCK_COLS))


def still_tables(wide, fields, basis_ref, pairs_ref, lin, raw, sums, rows, cols):
    dot = functools.partial(jnp.dot, preferred_element_type=F32)

    @pl.loop(0, cols // SPAN)
    def _(part):
        start = pl.multiple_of(part * SPAN, SPAN)

        def body(r, c, at):
            value, sx, sy = slopes_of(wide, r, at)
            here = (pl.ds(r, BLOCK_ROWS), pl.ds(c, BLOCK_COLS))
            for k, field in enumerate((value * sx, value * sy, sx, sy, sx * sx, sx * sy, sy * sy)):
                fields[(k, *here)] = field.astype(BF16)
            sums[1] += fold(value)
            sums[3] += fold(value * value)

        blocks(rows, start, body)
        cut = pl.ds(start, SPAN)
        for k in range(2):
            lin[1 + k] += dot(fields[2 * k], basis_ref[0, cut, :]) + dot(fields[2 * k + 1], basis_ref[1, cut, :])
        for k in range(3):
            raw[k] += dot(fields[4 + k], pairs_ref[0, cut, :]) + dot(fields[4 + k], pairs_ref[1, cut, :])


def rest_tables(wide, fixed, fixed_row, fields, basis_ref, lin, sums, rows, cols):
    dot = functools.partial(jnp.dot, preferred_element_type=F32)

    @pl.loop(0, cols // SPAN)
    def _(part):
        start = pl.multiple_of(part * SPAN, SPAN)

        def body(r, c, at):
            value, sx, sy = slopes_of(wide, r, at)
            f = fixed[pl.ds(pl.multiple_of(fixed_row + r, BLOCK_ROWS), BLOCK_ROWS), pl.ds(at, BLOCK_COLS)]
            f = f.astype(F32)
            rest = f - value
            here = (pl.ds(r, BLOCK_ROWS), pl.ds(c, BLOCK_COLS))
            fields[(0, *here)] = (rest * sx).astype(BF16)
            fields[(1, *here)] = (rest * sy).astype(BF16)
            sums[0] += fold(f)
            sums[2] += fold(rest * value)

        blocks(rows, start, body)
        cut = pl.ds(start, SPAN)
        here = pl.ds(0, rows)
        lin[0, here] += dot(fields[0, here], basis_ref[0, cut, :]) + dot(fields[1, here], basis_ref[1, cut, :])


def quad_tables(raw, quad):
    for d in range(BAND):
        at = slice(d * GRID_SIZE, (d + 1) * GRID_SIZE)
        xx, xy, yy = (raw[k, :, at] for k in range(3))
        quad[d] = jnp.concatenate([xx, yy], axis=1)
        quad[BAND + d] = jnp.concatenate([xy, xy], axis=1)


def head_rows(sums, keys):
    zero = jnp.zeros((1, LANES), F32)
    rows = [jnp.sum(sums[k], axis=0, keepdims=True) if k in keys else zero for k in range(4)]
    return jnp.concatenate(rows + [jnp.zeros((HEAD - 4, LANES), F32)], axis=0)


def grand(values):
    return jnp.sum(jnp.sum(values, axis=0, keepdims=True), axis=1, keepdims=True)


def track_kernel(strips, chain, m_ref, anchor_ref, acc_ref, mixed_ref, *scratch):
    (fixed, low, top, bottom, wide, fields, basis_ref, pairs_ref, lin, raw, quad, sums) = scratch[:12]
    (row_basis, row_basis_t, moved, hist, parts, side, near, ends, grads) = scratch[12:21]
    (quad_send, quad_recv, side_send, side_recv, near_send, near_recv) = scratch[21:27]
    (end_send, end_recv, bulk_send, bulk_recv, local_sem) = scratch[27:]
    rows, cols = m_ref.shape
    half = rows // 2
    me, link = lax.axis_index("quad"), lax.axis_index("chain")
    knots = GRID_SIZE // strips
    window = window_of(knots)
    spacing = rows * strips // GRID_SIZE
    pixel_count = float(rows * strips * cols)
    base = base_of(me, knots)
    first, last = link == 0, link == chain - 1
    steps = range(1, strips)

    def mesh_copy(src, dst, send, recv, to):
        return pltpu.make_async_remote_copy(
            src_ref=src, dst_ref=dst, send_sem=send, recv_sem=recv, device_id=to, device_id_type=MESH
        )

    barrier = pltpu.get_barrier_semaphore()

    def greet(to):
        pl.semaphore_signal(barrier, inc=1, device_id=to, device_id_type=MESH)

    for step in steps:
        greet({"quad": lax.rem(me + step, strips)})
    for step in range(1, chain):
        greet({"chain": lax.rem(link + step, chain)})
    for edge, to in ((last, link + 1), (first, link - 1)):

        @pl.when(jnp.logical_not(edge))
        def _():
            for step in steps:
                greet({"chain": to, "quad": lax.rem(me + step, strips)})

    load_anchor = pltpu.make_async_copy(anchor_ref, fixed, local_sem)

    @pl.when(first)
    def _():
        load_anchor.start()

    @pl.when(me == 0)
    def _():
        top[...] = jnp.zeros_like(top)

    @pl.when(me == strips - 1)
    def _():
        bottom[...] = jnp.zeros_like(bottom)
        low[pl.ds(HALO + half, HALO), :] = jnp.zeros((HALO, cols), BF16)

    @pl.when(first)
    def _():
        near[:, 0] = jnp.zeros_like(near[:, 0])
        side[...] = jnp.zeros_like(side)

    @pl.when(last)
    def _():
        near[:, 1] = jnp.zeros_like(near[:, 1])

    begin = me * rows
    row_basis[...] = strip_basis((rows, window), 0, begin, base - 8, spacing)
    row_basis_t[...] = strip_basis((window, rows), 1, begin, base - 8, spacing)
    for ref in (hist, grads, lin, raw, sums):
        ref[...] = jnp.zeros_like(ref)
    zeros = jnp.zeros((rows + 2 * EDGE, LANES), F32)
    wide[:, pl.ds(0, LANES)] = zeros
    wide[:, pl.ds(cols + LANES, LANES)] = zeros
    column_tables(basis_ref, pairs_ref, cols // GRID_SIZE)
    cross = jnp.where(first, 0, strips - 1) + jnp.where(last, 0, strips - 1)
    pl.semaphore_wait(barrier, strips - 1 + chain - 1 + cross)

    start_rows, end_rows = m_ref.at[pl.ds(0, HALO)], m_ref.at[pl.ds(rows - HALO, HALO)]
    to_top = mesh_copy(end_rows, top, bulk_send.at[0], bulk_recv.at[0], {"quad": me + 1})
    to_bottom = mesh_copy(start_rows, bottom, bulk_send.at[1], bulk_recv.at[1], {"quad": me - 1})
    up = mesh_copy(
        m_ref.at[pl.ds(0, half)], fixed.at[pl.ds(0, half)], bulk_send.at[2], bulk_recv.at[2], {"chain": link + 1}
    )
    down = mesh_copy(
        m_ref.at[pl.ds(half - HALO, half + HALO)],
        low.at[pl.ds(0, half + HALO)],
        bulk_send.at[3],
        bulk_recv.at[3],
        {"chain": link - 1},
    )
    across = mesh_copy(
        start_rows,
        low.at[pl.ds(HALO + half, HALO)],
        bulk_send.at[4],
        bulk_recv.at[4],
        {"chain": link - 1, "quad": me - 1},
    )
    inner_top, inner_bottom = me > 0, me < strips - 1
    later, earlier = jnp.logical_not(last), jnp.logical_not(first)
    pl.when(inner_bottom)(lambda: to_top.start())
    pl.when(inner_top)(lambda: to_bottom.start())
    pl.when(later)(lambda: up.start())
    pl.when(earlier)(lambda: down.start())
    pl.when(jnp.logical_and(earlier, inner_top))(lambda: across.start())

    fill_body(wide, m_ref, 0, rows)
    pl.when(inner_top)(lambda: to_top.wait_recv())
    pl.when(inner_bottom)(lambda: to_bottom.wait_recv())
    fill_rows(wide, 0, top, 0, EDGE, EDGE)
    wide[pl.ds(EDGE + rows, EDGE), pl.ds(LANES, cols)] = bottom[...].astype(F32)[:EDGE]

    still_tables(wide, fields, basis_ref, pairs_ref, lin, raw, sums, rows, cols)
    quad_tables(raw, quad)

    exact = functools.partial(jnp.dot, precision=EXACT, preferred_element_type=F32)

    @pl.when(first)
    def _():
        load_anchor.wait()
        rest_tables(wide, fixed, 0, fields, basis_ref, lin, sums, rows, cols)

    @pl.when(earlier)
    def _():
        up.wait_recv()
        rest_tables(wide, fixed, 0, fields, basis_ref, lin, sums, half, cols)

    parts[0, me, pl.ds(0, HEAD)] = head_rows(sums, (0, 1, 2, 3))
    for k in range(3):
        parts[0, me, pl.ds(HEAD + k * window, window)] = exact(row_basis_t[...], lin[k])

    def spread(turn, count):
        copies = []
        for step in steps:
            at = parts.at[turn, me, pl.ds(0, count)]
            to = {"quad": lax.rem(me + step, strips)}
            copies.append(mesh_copy(at, at, quad_send.at[turn, step], quad_recv.at[turn, me], to))
        for copy in copies:
            copy.start()
        return copies

    def gathered(turn, count):
        for step in steps:
            peer = lax.rem(me + step, strips)
            at = parts.at[turn, peer, pl.ds(0, count)]
            mesh_copy(at, at, quad_send.at[turn, step], quad_recv.at[turn, peer], {"quad": peer}).wait_recv()

    def side_copy(row, step):
        to = {"chain": link + 1, "quad": lax.rem(me + step, strips)}
        return mesh_copy(parts.at[ITERATIONS, me, pl.ds(0, HEAD + window)], side.at[row], side_send.at[step], side_recv.at[row], to)

    sends = spread(0, HEAD + 3 * window)

    @pl.when(later)
    def _():
        down.wait_recv()
        pl.when(inner_bottom)(lambda: across.wait_recv())
        fill_body(wide, low, HALO, half)
        fill_rows(wide, 0, low, 0, EDGE, EDGE)
        tail = low[pl.ds(HALO + half, HALO), :].astype(F32)
        wide[pl.ds(EDGE + half, EDGE), pl.ds(LANES, cols)] = tail[:EDGE]
        sums[...] = jnp.zeros_like(sums)
        lin[0] = jnp.zeros_like(lin[0])
        rest_tables(wide, m_ref, half, fields, basis_ref, lin, sums, half, cols)
        parts[ITERATIONS, me, pl.ds(0, HEAD)] = head_rows(sums, (0, 2))
        parts[ITERATIONS, me, pl.ds(HEAD, window)] = exact(row_basis_t[:, half:], lin[0, pl.ds(0, half)])
        for step in range(strips):
            side_copy(me, step).start()

    gathered(0, HEAD + 3 * window)

    @pl.when(earlier)
    def _():
        for step in range(strips):
            side_copy(lax.rem(me + step, strips), step).wait_recv()

    def near_copy(turn, side_of):
        to = {"chain": link + 1 if side_of == 0 else link - 1}
        src = hist.at[turn, pl.ds(8, GRID_SIZE)]
        return mesh_copy(src, near.at[turn, side_of], near_send.at[turn, side_of], near_recv.at[turn, side_of], to)

    def collect(ref, turn, offset, slot):
        for strip in range(strips):
            at = strip * knots // 8 * 8
            here = (strip, pl.ds(offset, window))
            grads[slot, pl.ds(at, window)] += ref[here] if turn is None else ref[(turn, *here)]
        return grads[slot, pl.ds(8, GRID_SIZE)]

    head = parts[0, 0, pl.ds(0, HEAD)] + side[0, pl.ds(0, HEAD)]
    for strip in steps:
        head = head + (parts[0, strip, pl.ds(0, HEAD)] + side[strip, pl.ds(0, HEAD)])
    head = jnp.sum(head, axis=1, keepdims=True)
    total = [head[k : k + 1, :] for k in range(4)]
    collect(side, None, HEAD, 0)
    grad_rest, grad_still, grad_ones = (collect(parts, 0, HEAD + k * window, k) for k in range(3))
    fixed_mean = total[0] / pixel_count
    block = 128

    for turn in range(ITERATIONS):
        moving_sum, moving_sq, cross_sum = total[1], total[3], total[2] + total[3]
        grad_extra = 0.0
        before = hist[turn, pl.ds(8, GRID_SIZE)]
        smooth = 0.0
        if turn:
            mixed_all = exact(row_basis[...], hist[turn, pl.ds(base, window)])
            moved[...] = mixed_all.astype(BF16).astype(F32)

            @pl.loop(0, rows // block)
            def _(i):
                r = pl.ds(pl.multiple_of(i * block, block), block)
                mixed = moved[r, :]
                other = pltpu.roll(mixed, GRID_SIZE, 1)
                out = quad[0, r, :] * mixed + quad[BAND, r, :] * other
                for d in range(1, BAND):
                    q, p = quad[d, r, :], quad[BAND + d, r, :]
                    out += q * pltpu.roll(mixed, LANES - d, 1) + p * pltpu.roll(other, LANES - d, 1)
                    out += pltpu.roll(q * mixed + p * other, d, 1)
                moved[r, :] = out

            parts[turn, me, pl.ds(0, window)] = exact(row_basis_t[...], moved[...])
            sends += spread(turn, window)
            gathered(turn, window)
            grad_extra = collect(parts, turn, 0, 2 + turn)
            moving_sum = moving_sum + grand(before * grad_ones)
            moving_sq = moving_sq + grand(before * (2.0 * grad_still + grad_extra))
            cross_sum = cross_sum + grand(before * (grad_rest + grad_still))
            pl.when(earlier)(lambda: near_copy(turn, 0).wait_recv())
            pl.when(later)(lambda: near_copy(turn, 1).wait_recv())
            smooth = near[turn, 0] - 2.0 * before + near[turn, 1]
        moving_mean = moving_sum / pixel_count
        moving_var = moving_sq - pixel_count * moving_mean * moving_mean
        cross_var = cross_sum - pixel_count * fixed_mean * moving_mean
        denominator = jnp.sqrt(moving_var + EPSILON)
        ratio = cross_var / denominator / (moving_var + EPSILON)
        gradient = pixel_count * (
            (grad_rest + grad_still - fixed_mean * grad_ones) / denominator
            - ratio * (grad_still + grad_extra - moving_mean * grad_ones)
        )
        size = grand(gradient * gradient) / (2.0 * GRID_SIZE * GRID_SIZE)
        direction = gradient / jnp.sqrt(size + EPSILON)
        hist[turn + 1, pl.ds(8, GRID_SIZE)] = before + direction / ITERATIONS + SMOOTHING * smooth
        if turn < ITERATIONS - 1:
            pl.when(later)(lambda: near_copy(turn + 1, 0).start())
            pl.when(earlier)(lambda: near_copy(turn + 1, 1).start())

    def end_copy(owner, step):
        src = hist.at[ITERATIONS, pl.ds(8, GRID_SIZE)]
        to = {"chain": lax.rem(link + step, chain)}
        return mesh_copy(src, ends.at[owner], end_send.at[step], end_recv.at[owner], to)

    for step in range(1, chain):
        end_copy(link, step).start()
    ends[link] = hist[ITERATIONS, pl.ds(8, GRID_SIZE)]
    for step in range(1, chain):
        end_copy(lax.rem(link + step, chain), step).wait_recv()
    out = ends[0]
    for owner in range(1, chain):
        out = out + jnp.where(owner <= link, ends[owner], 0.0)
    acc_ref[...] = out
    hist[0, pl.ds(8, GRID_SIZE)] = out
    mixed_ref[...] = exact(row_basis[...], hist[0, pl.ds(base, window)]).astype(BF16)
    for copy in sends:
        copy.wait_send()
    for turn in range(1, ITERATIONS):
        pl.when(later)(lambda: near_copy(turn, 0).wait_send())
        pl.when(earlier)(lambda: near_copy(turn, 1).wait_send())
    for step in range(1, chain):
        end_copy(link, step).wait_send()
    pl.when(inner_bottom)(lambda: to_top.wait_send())
    pl.when(inner_top)(lambda: to_bottom.wait_send())
    pl.when(earlier)(lambda: down.wait_send())
    pl.when(jnp.logical_and(earlier, inner_top))(lambda: across.wait_send())

    @pl.when(later)
    def _():
        up.wait_send()
        for step in range(strips):
            side_copy(me, step).wait_send()


def track(moving, anchor):
    rows, cols = moving.shape
    strips, chain = lax.axis_size("quad"), lax.axis_size("chain")
    window = window_of(GRID_SIZE // strips)
    vmem = pl.BlockSpec(memory_space=pltpu.VMEM)
    tall = GRID_SIZE + 16 + window
    dma = pltpu.SemaphoreType.DMA
    return pl.pallas_call(
        functools.partial(track_kernel, strips, chain),
        out_shape=(
            jax.ShapeDtypeStruct((GRID_SIZE, LANES), F32),
            jax.ShapeDtypeStruct((rows, LANES), BF16),
        ),
        in_specs=[vmem, pl.BlockSpec(memory_space=pl.ANY)],
        out_specs=[vmem] * 2,
        scratch_shapes=[
            pltpu.VMEM((rows, cols), BF16),
            pltpu.VMEM((rows // 2 + 2 * HALO, cols), BF16),
            pltpu.VMEM((HALO, cols), BF16),
            pltpu.VMEM((HALO, cols), BF16),
            pltpu.VMEM((rows + 2 * EDGE, cols + 2 * LANES), F32),
            pltpu.VMEM((FIELDS, rows, SPAN), BF16),
            pltpu.VMEM((2, cols, LANES), BF16),
            pltpu.VMEM((2, cols, BAND * GRID_SIZE), BF16),
            pltpu.VMEM((3, rows, LANES), F32),
            pltpu.VMEM((3, rows, BAND * GRID_SIZE), F32),
            pltpu.VMEM((2 * BAND, rows, LANES), F32),
            pltpu.VMEM((4, 8, LANES), F32),
            pltpu.VMEM((rows, window), F32),
            pltpu.VMEM((window, rows), F32),
            pltpu.VMEM((rows, LANES), F32),
            pltpu.VMEM((ITERATIONS + 1, tall, LANES), F32),
            pltpu.VMEM((ITERATIONS + 1, strips, HEAD + 3 * window, LANES), F32),
            pltpu.VMEM((strips, HEAD + window, LANES), F32),
            pltpu.VMEM((ITERATIONS + 1, 2, GRID_SIZE, LANES), F32),
            pltpu.VMEM((chain, GRID_SIZE, LANES), F32),
            pltpu.VMEM((ITERATIONS + 2, tall, LANES), F32),
            dma((ITERATIONS, strips)),
            dma((ITERATIONS, strips)),
            dma((strips,)),
            dma((strips,)),
            dma((ITERATIONS + 1, 2)),
            dma((ITERATIONS + 1, 2)),
            dma((chain,)),
            dma((chain,)),
            dma((5,)),
            dma((5,)),
            dma,
        ],
        compiler_params=pltpu.CompilerParams(
            collective_id=0, has_side_effects=True, vmem_limit_bytes=VMEM_BYTES
        ),
    )(moving, anchor)


def local(sections, anchor):
    _, rows, columns = sections.shape
    moving = sections[0]
    basis = spline_basis(0, columns, columns).astype(jnp.bfloat16)
    before, after = with_ends(moving, "quad", 0)
    edges = jnp.concatenate(
        [
            jnp.broadcast_to(before, (EDGE, columns)),
            jnp.broadcast_to(after, (EDGE, columns)),
        ],
        axis=0,
    ).astype(jnp.float32)
    accumulated, mixed = track(moving, anchor)
    registered = warp(moving, edges, mixed, basis.T)
    return registered[None], accumulated[None]


def solution(mesh):
    in_specs = (P("chain", "quad", None), P("quad", None))
    out_specs = (P("chain", "quad", None), P("chain", None, None))
    return jax.shard_map(local, mesh=mesh, in_specs=in_specs, out_specs=out_specs, check_vma=False)
```

time: 394 us -> 137 us (0.35)
  blocking collectives: 113 us -> 0 us
  waiting for transfers between devices: 98.4 us -> 0.01 us
  Pallas kernels: 69.3 us -> 126 us
  between operations: 33.6 us -> 0.7 us
  other arithmetic: 34 us -> 2.29 us
  local copies, waits for them, and re-layouts: 16.4 us -> 1.54 us
  starting transfers between devices: 17.9 us -> 6.19 us
  matrix products: 10.9 us -> 0 us
    psum x3 -> x0, blocking collectives: 105 us -> none  [local(): grad_extra, scalars = lax.psum((gather(moved), scalars), 'quad')]
    psum x1 -> x0, waiting for transfers between devices: 92.3 us -> none  [local(): lax.psum((gather(lin[0]), gather(lin[1]), gather(lin[2]), totals), 'quad')]
    pallas_call x1, Pallas kernels: 45.4 us -> 102 us  [track(): pl.pallas_call(functools.partial(track_kernel, strips, chain), out_shape=...]
    slice x37 -> x0, local copies, waits for them, and re-layouts: 13.2 us -> none  [the longest x3 5.89 us: local(): wide_basis[:, d:]]
    dot_general x10 -> x0, matrix products: 10.9 us -> none  [the longest x1 2.38 us: local(): gather(lin[2])]
    another operation x5 -> x0, other arithmetic: 10.4 us -> none  [the longest x3 5.91 us: local(): jnp.stack([jnp.sum(mixed * lin[2]), jnp.sum(mixed * (2.0 * lin[1] + moved...]
    concatenate x11 -> x0, other arithmetic: 8.08 us -> none  [the longest x2 6.24 us: local(): jnp.concatenate([wide_basis * jnp.pad(wide_basis[:, d:], ((0, 0), (0, d))...]
    reduce_sum x9 -> x0, other arithmetic: 7.9 us -> none  [the longest x3 3.93 us: local(): jnp.sum(mixed * lin[2])]
  transfers between devices with their start and end apart: 10 -> 2, of which waited for: 4 -> 0; matrix products, arithmetic and copies ran while one was open for 6% -> 1% of each run, Pallas kernels for 0% -> 75%
where the time goes in v1:
time: 137 us
  Pallas kernels  126 us (92%)
  starting transfers between devices  6.19 us (5%)
  other arithmetic  2.29 us (2%)
  local copies, waits for them, and re-layouts  1.54 us (1%)
    pallas_call x1, Pallas kernels, track(): pl.pallas_call(functools.partial(track_kernel, strips, chain), out_shape=...  102 us
    pallas_call x1, Pallas kernels, warp(): pl.pallas_call(warp_kernel, out_shape=jax.ShapeDtypeStruct((rows, cols),...  23.9 us
    ppermute x1, starting transfers between devices, with_ends(): lax.ppermute(lax.slice_in_dim(array, length - 1, length, axis=dim), axis,...  4.9 us
  transfers between devices with their start and end apart: 2, of which 0 were waited for; matrix products, arithmetic and copies ran while one was open for 1% of the time, Pallas kernels for 75%

profile of v1, /device:TPU:0, one launch (start us, length us, event | category | flops | bytes accessed | tf_op | source)
XLA Modules:
  0.0 137.1 jit_solution(89901541270530363)
XLA Ops:
  0.6 0.9 slice_bitcast_fusion.1
  1.5 4.9 %collective-permute-start = (bf16[1,4096]{1,0:T(2,128)(2,1)S(1)}, bf16[1,4096]{1,0:T(2,128)(2,1)S(1)}, u32[]{:S(2)}, u32[]{:S(2)}) collective-permute-start(bf16[1,4096]{1,0:T(2,128)(2,1)S(1)} %get-tuple-element.6), channel_id=1, source_target_pairs={{0,1},{1,2},{2,3},{3,4},{4,5},{5,6},{6,7},{8,9},{9,10},{10,11},{11... | collective-permute-start | bytes 24584 | tf_op jit(solution)/shard_map/ppermute | solution.py:44
  6.4 1.3 collective-permute-start.1
  7.8 1.4 %fusion.2.flat_ref = bf16[64,4096]{1,0:T(8,128)(2,1)} fusion(f32[64]{0:T(128)S(1)} %iota_convert_fusion, f32[4096]{0:T(1024)S(1)} %add_multiply_fusion), kind=kLoop, calls=%fused_computation.4 | loop fusion | flops 4718592 | bytes 540928 | tf_op jit(solution)/shard_map/convert_element_type | solution.py:610
  9.2 102.4 %shard_map.41 = (f32[64,128]{1,0:T(8,128)}, bf16[512,128]{1,0:T(8,128)(2,1)}) custom-call(bf16[512,4096]{1,0:T(8,128)(2,1)} %bitcast.7, bf16[512,4096]{1,0:T(8,128)(2,1)} %anchor_ref.1), custom_call_target="tpu_custom_call" | custom-call | tf_op jit(solution)/shard_map/pallas_call | solution.py:559
  111.7 0.0 collective-permute-done
  111.7 0.1 reduce
  111.7 0.0 collective-permute-done.1
  111.7 0.1 reduce.1
  111.8 0.7 maximum_convert_fusion.edges_ref
  112.5 0.0 copy-start
  112.5 23.9 %shard_map.42 = bf16[512,4096]{1,0:T(8,128)(2,1)} custom-call(bf16[512,4096]{1,0:T(8,128)(2,1)} %bitcast.8, f32[16,4096]{1,0:T(8,128)} %maximum_convert_fusion.edges_ref, bf16[512,128]{1,0:T(8,128)(2,1)} %get-tuple-element.4.mixed_ref, bf16[64,4096]{1,0:T(8,128)(2,1)} %fusion.2.flat_ref), custom_call_target="tpu_custom_call" | custom-call | tf_op jit(solution)/shard_map/pallas_call | solution.py:117
  136.4 0.0 copy-done
  136.5 0.6 copy.5
  (4 shorter events, 0.0 us)
Async XLA Ops:
  1.5 110.1 %collective-permute-start = (bf16[1,4096]{1,0:T(2,128)(2,1)S(1)}, bf16[1,4096]{1,0:T(2,128)(2,1)S(1)}, u32[]{:S(2)}, u32[]{:S(2)}) collective-permute-start(bf16[1,4096]{1,0:T(2,128)(2,1)S(1)} %get-tuple-element.6), channel_id=1, source_target_pairs={{0,1},{1,2},{2,3},{3,4},{4,5},{5,6},{6,7},{8,9},{9,10},{10,11},{11... | collective-permute-start | bytes 24584 | tf_op jit(solution)/shard_map/ppermute | solution.py:44
  6.4 105.3 %collective-permute-start.1 = (bf16[1,4096]{1,0:T(2,128)(2,1)S(1)}, bf16[1,4096]{1,0:T(2,128)(2,1)S(1)}, u32[]{:S(2)}, u32[]{:S(2)}) collective-permute-start(bf16[1,4096]{1,0:T(2,128)(2,1)S(1)} %get-tuple-element.7), channel_id=1, source_target_pairs={{1,0},{2,1},{3,2},{4,3},{5,4},{6,5},{7,6},{9,8},{10,9},{11,10},{12... | collective-permute-start | bytes 24584 | tf_op jit(solution)/shard_map/ppermute | solution.py:45
  112.5 23.9 %copy-start = (f32[64,128]{1,0:T(8,128)S(1)}, f32[64,128]{1,0:T(8,128)}, u32[]{:S(2)}) copy-start(f32[64,128]{1,0:T(8,128)} %get-tuple-element.5) | copy-start | bytes 98308

commit v2 on v1

--- a/solution.py
+++ b/solution.py
@@ -2,6 +2,7 @@
 
 import jax
 import jax.numpy as jnp
+import numpy as np
 from jax import lax
 from jax.experimental import pallas as pl
 from jax.experimental.pallas import tpu as pltpu
@@ -16,8 +17,8 @@
 SPLIT = 4
 LANES = 128
 EDGE = 8
-BLOCK_ROWS = 32
-BLOCK_COLS = 512
+BLOCK_ROWS = 64
+BLOCK_COLS = 1024
 VMEM_BYTES = 60 * 2**20
 
 
@@ -29,49 +30,15 @@
     return jnp.where(distance < 1.0, near_part, jnp.where(distance < 2.0, far_part, 0.0))
 
 
-def spline_basis(first_row, pixel_count, extent):
-    spacing = extent // GRID_SIZE
-    pixels = (first_row + jnp.arange(pixel_count, dtype=jnp.int32)).astype(jnp.float32)
-    knot_pos = jnp.arange(GRID_SIZE, dtype=jnp.int32).astype(jnp.float32)
-    offset = (pixels[:, None] + 0.5) / spacing - knot_pos[None, :] - 0.5
-    return spline_weight(offset)
-
-
-def with_ends(array, axis, dim):
-    size, length = lax.axis_size(axis), array.shape[dim]
-    up = [(i, i + 1) for i in range(size - 1)]
-    down = [(j, i) for i, j in up]
-    before = lax.ppermute(lax.slice_in_dim(array, length - 1, length, axis=dim), axis, up)
-    after = lax.ppermute(lax.slice_in_dim(array, 0, 1, axis=dim), axis, down)
-    return before, after
-
-
-def fill_wide(m_ref, edges_ref, wide):
-    rows, cols = m_ref.shape
-    height = rows + 2 * EDGE
-    zeros = jnp.zeros((height, LANES), jnp.float32)
-    wide[:, pl.ds(0, LANES)] = zeros
-    wide[:, pl.ds(cols + LANES, LANES)] = zeros
-    wide[pl.ds(0, EDGE), pl.ds(LANES, cols)] = edges_ref[pl.ds(0, EDGE), :]
-    wide[pl.ds(EDGE + rows, EDGE), pl.ds(LANES, cols)] = edges_ref[pl.ds(EDGE, EDGE), :]
-
-    @pl.loop(0, rows // BLOCK_ROWS)
-    def _(i):
-        r = pl.multiple_of(i * BLOCK_ROWS, BLOCK_ROWS)
-        wide[pl.ds(EDGE + r, BLOCK_ROWS), pl.ds(LANES, cols)] = m_ref[
-            pl.ds(r, BLOCK_ROWS), :
-        ].astype(jnp.float32)
-
-
 def slopes_of(wide, r, c):
     across = wide[pl.ds(r + EDGE, BLOCK_ROWS), pl.ds(c, BLOCK_COLS + 2 * LANES)]
     total = BLOCK_COLS + 2 * LANES
-    slope_x = 0.5 * (pltpu.roll(across, total - 1, 1) - pltpu.roll(across, 1, 1))
+    slope_x = pltpu.roll(across, total - 1, 1) - pltpu.roll(across, 1, 1)
     slope_x = slope_x[:, LANES : LANES + BLOCK_COLS]
     value = across[:, LANES : LANES + BLOCK_COLS]
     down = wide[pl.ds(r, BLOCK_ROWS + 2 * EDGE), pl.ds(c + LANES, BLOCK_COLS)]
     tall = BLOCK_ROWS + 2 * EDGE
-    slope_y = 0.5 * (pltpu.roll(down, tall - 1, 0) - pltpu.roll(down, 1, 0))
+    slope_y = pltpu.roll(down, tall - 1, 0) - pltpu.roll(down, 1, 0)
     slope_y = slope_y[EDGE : EDGE + BLOCK_ROWS, :]
     return value, slope_x, slope_y
 
@@ -85,47 +52,51 @@
     return out
 
 
-def warp_kernel(m_ref, edges_ref, mixed_ref, flat_ref, out_ref, wide, stage_x, stage_y):
-    rows, cols = m_ref.shape
-    fill_wide(m_ref, edges_ref, wide)
-    span = stage_x.shape[1]
-
-    @pl.loop(0, cols // span)
-    def _(chunk):
-        start = pl.multiple_of(chunk * span, span)
-        flat = flat_ref[:, pl.ds(start, span)]
-        stage_x[...] = jnp.dot(mixed_ref[:, :GRID_SIZE], flat, preferred_element_type=jnp.float32)
-        stage_y[...] = jnp.dot(mixed_ref[:, GRID_SIZE:], flat, preferred_element_type=jnp.float32)
-        per_row = span // BLOCK_COLS
-
-        @pl.loop(0, rows // BLOCK_ROWS * per_row)
-        def _(step):
-            i, j = step // per_row, step % per_row
-            r = pl.multiple_of(i * BLOCK_ROWS, BLOCK_ROWS)
-            c = pl.multiple_of(j * BLOCK_COLS, BLOCK_COLS)
-            value, sx, sy = slopes_of(wide, r, pl.multiple_of(start + c, BLOCK_COLS))
-            here = (pl.ds(r, BLOCK_ROWS), pl.ds(c, BLOCK_COLS))
-            out = value + stage_x[here] * sx + stage_y[here] * sy
-            out_ref[pl.ds(r, BLOCK_ROWS), pl.ds(pl.multiple_of(start + c, BLOCK_COLS), BLOCK_COLS)] = (
-                out.astype(jnp.bfloat16)
-            )
+def warp_kernel(above_ref, m_ref, below_ref, edges_ref, mixed_ref, flat_ref, out_ref, wide):
+    step, rows, cols = pl.program_id(0), m_ref.shape[0], m_ref.shape[1]
+    zeros = jnp.zeros((rows + 2 * EDGE, LANES), jnp.float32)
+    wide[:, pl.ds(0, LANES)] = zeros
+    wide[:, pl.ds(cols + LANES, LANES)] = zeros
+    above = above_ref[...].astype(jnp.float32)[EDGE:]
+    below = below_ref[...].astype(jnp.float32)[:EDGE]
+    inner = pl.ds(LANES, cols)
+    wide[pl.ds(0, EDGE), inner] = jnp.where(step == 0, edges_ref[pl.ds(0, EDGE), :], above)
+    wide[pl.ds(EDGE + rows, EDGE), inner] = jnp.where(
+        step == pl.num_programs(0) - 1, edges_ref[pl.ds(EDGE, EDGE), :], below
+    )
+    wide[pl.ds(EDGE, rows), inner] = m_ref[...].astype(jnp.float32)
+
+    @pl.loop(0, cols // BLOCK_COLS)
+    def _(j):
+        c = pl.multiple_of(j * BLOCK_COLS, BLOCK_COLS)
+        value, sx, sy = slopes_of(wide, 0, c)
+        flat = flat_ref[:, pl.ds(c, BLOCK_COLS)]
+        shift_x = jnp.dot(mixed_ref[:, :GRID_SIZE], flat, preferred_element_type=jnp.float32)
+        shift_y = jnp.dot(mixed_ref[:, GRID_SIZE:], flat, preferred_element_type=jnp.float32)
+        out_ref[:, pl.ds(c, BLOCK_COLS)] = (value + shift_x * sx + shift_y * sy).astype(jnp.bfloat16)
 
 
 def warp(moving, edges, mixed, flat):
     rows, cols = moving.shape
-    vmem = pl.BlockSpec(memory_space=pltpu.VMEM)
+    thin = 2 * EDGE
+    ratio, last = BLOCK_ROWS // thin, rows // thin - 1
+    whole = lambda shape: pl.BlockSpec(shape, lambda i: (0, 0))
     return pl.pallas_call(
         warp_kernel,
+        grid=(rows // BLOCK_ROWS,),
         out_shape=jax.ShapeDtypeStruct((rows, cols), jnp.bfloat16),
-        in_specs=[vmem] * 4,
-        out_specs=vmem,
-        scratch_shapes=[
-            pltpu.VMEM((rows + 2 * EDGE, cols + 2 * LANES), jnp.float32),
-            pltpu.VMEM((rows, 1024), jnp.float32),
-            pltpu.VMEM((rows, 1024), jnp.float32),
+        in_specs=[
+            pl.BlockSpec((thin, cols), lambda i: (jnp.maximum(ratio * i - 1, 0), 0)),
+            pl.BlockSpec((BLOCK_ROWS, cols), lambda i: (i, 0)),
+            pl.BlockSpec((thin, cols), lambda i: (jnp.minimum(ratio * i + ratio, last), 0)),
+            whole(edges.shape),
+            pl.BlockSpec((BLOCK_ROWS, LANES), lambda i: (i, 0)),
+            whole(flat.shape),
         ],
+        out_specs=pl.BlockSpec((BLOCK_ROWS, cols), lambda i: (i, 0)),
+        scratch_shapes=[pltpu.VMEM((BLOCK_ROWS + 2 * EDGE, cols + 2 * LANES), jnp.float32)],
         compiler_params=pltpu.CompilerParams(vmem_limit_bytes=VMEM_BYTES),
-    )(moving, edges, mixed, flat)
+    )(moving, moving, moving, edges, mixed, flat)
 
 
 MESH = pl.DeviceIdType.MESH
@@ -143,6 +114,17 @@
 
 def base_of(strip, knots):
     return lax.div(strip * knots, 8) * 8
+
+
+def flat_table(cols):
+    pixels = np.arange(cols, dtype=np.float32)[None, :]
+    knots = np.arange(GRID_SIZE, dtype=np.float32)[:, None]
+    offset = (pixels + np.float32(0.5)) / np.float32(cols // GRID_SIZE) - knots - np.float32(0.5)
+    distance = np.abs(offset)
+    near = np.float32(2.0 / 3.0) - distance * distance + np.float32(0.5) * distance * distance * distance
+    remain = np.float32(2.0) - distance
+    far = remain * remain * remain / np.float32(6.0)
+    return np.where(distance < 1, near, np.where(distance < 2, far, np.float32(0))).astype(BF16)
 
 
 def strip_basis(shape, pixel_dim, first_row, first_knot, spacing):
@@ -259,7 +241,7 @@
 def quad_tables(raw, quad):
     for d in range(BAND):
         at = slice(d * GRID_SIZE, (d + 1) * GRID_SIZE)
-        xx, xy, yy = (raw[k, :, at] for k in range(3))
+        xx, xy, yy = (0.25 * raw[k, :, at] for k in range(3))
         quad[d] = jnp.concatenate([xx, yy], axis=1)
         quad[BAND + d] = jnp.concatenate([xy, xy], axis=1)
 
@@ -274,7 +256,7 @@
     return jnp.sum(jnp.sum(values, axis=0, keepdims=True), axis=1, keepdims=True)
 
 
-def track_kernel(strips, chain, m_ref, anchor_ref, acc_ref, mixed_ref, *scratch):
+def track_kernel(strips, chain, m_ref, anchor_ref, acc_ref, mixed_ref, edges_ref, *scratch):
     (fixed, low, top, bottom, wide, fields, basis_ref, pairs_ref, lin, raw, quad, sums) = scratch[:12]
     (row_basis, row_basis_t, moved, hist, parts, side, near, ends, grads) = scratch[12:21]
     (quad_send, quad_recv, side_send, side_recv, near_send, near_recv) = scratch[21:27]
@@ -378,8 +360,9 @@
     fill_body(wide, m_ref, 0, rows)
     pl.when(inner_top)(lambda: to_top.wait_recv())
     pl.when(inner_bottom)(lambda: to_bottom.wait_recv())
-    fill_rows(wide, 0, top, 0, EDGE, EDGE)
-    wide[pl.ds(EDGE + rows, EDGE), pl.ds(LANES, cols)] = bottom[...].astype(F32)[:EDGE]
+    for k, values in enumerate((top[...].astype(F32)[EDGE:], bottom[...].astype(F32)[:EDGE])):
+        edges_ref[pl.ds(k * EDGE, EDGE), :] = values
+        wide[pl.ds(k * (EDGE + rows), EDGE), pl.ds(LANES, cols)] = values
 
     still_tables(wide, fields, basis_ref, pairs_ref, lin, raw, sums, rows, cols)
     quad_tables(raw, quad)
@@ -398,7 +381,7 @@
 
     parts[0, me, pl.ds(0, HEAD)] = head_rows(sums, (0, 1, 2, 3))
     for k in range(3):
-        parts[0, me, pl.ds(HEAD + k * window, window)] = exact(row_basis_t[...], lin[k])
+        parts[0, me, pl.ds(HEAD + k * window, window)] = 0.5 * exact(row_basis_t[...], lin[k])
 
     def spread(turn, count):
         copies = []
@@ -434,7 +417,7 @@
         lin[0] = jnp.zeros_like(lin[0])
         rest_tables(wide, m_ref, half, fields, basis_ref, lin, sums, half, cols)
         parts[ITERATIONS, me, pl.ds(0, HEAD)] = head_rows(sums, (0, 2))
-        parts[ITERATIONS, me, pl.ds(HEAD, window)] = exact(row_basis_t[:, half:], lin[0, pl.ds(0, half)])
+        parts[ITERATIONS, me, pl.ds(HEAD, window)] = 0.5 * exact(row_basis_t[:, half:], lin[0, pl.ds(0, half)])
         for step in range(strips):
             side_copy(me, step).start()
 
@@ -529,7 +512,7 @@
         out = out + jnp.where(owner <= link, ends[owner], 0.0)
     acc_ref[...] = out
     hist[0, pl.ds(8, GRID_SIZE)] = out
-    mixed_ref[...] = exact(row_basis[...], hist[0, pl.ds(base, window)]).astype(BF16)
+    mixed_ref[...] = exact(row_basis[...], hist[0, pl.ds(base, window)]).astype(BF16) * jnp.asarray(0.5, BF16)
     for copy in sends:
         copy.wait_send()
     for turn in range(1, ITERATIONS):
@@ -561,9 +544,10 @@
         out_shape=(
             jax.ShapeDtypeStruct((GRID_SIZE, LANES), F32),
             jax.ShapeDtypeStruct((rows, LANES), BF16),
+            jax.ShapeDtypeStruct((2 * EDGE, cols), F32),
         ),
         in_specs=[vmem, pl.BlockSpec(memory_space=pl.ANY)],
-        out_specs=[vmem] * 2,
+        out_specs=[vmem] * 3,
         scratch_shapes=[
             pltpu.VMEM((rows, cols), BF16),
             pltpu.VMEM((rows // 2 + 2 * HALO, cols), BF16),
@@ -605,19 +589,9 @@
 
 
 def local(sections, anchor):
-    _, rows, columns = sections.shape
     moving = sections[0]
-    basis = spline_basis(0, columns, columns).astype(jnp.bfloat16)
-    before, after = with_ends(moving, "quad", 0)
-    edges = jnp.concatenate(
-        [
-            jnp.broadcast_to(before, (EDGE, columns)),
-            jnp.broadcast_to(after, (EDGE, columns)),
-        ],
-        axis=0,
-    ).astype(jnp.float32)
-    accumulated, mixed = track(moving, anchor)
-    registered = warp(moving, edges, mixed, basis.T)
+    accumulated, mixed, edges = track(moving, anchor)
+    registered = warp(moving, edges, mixed, flat_table(moving.shape[1]))
     return registered[None], accumulated[None]
 
 

time: 137 us -> 98.6 us (0.72)
  Pallas kernels: 126 us -> 97.1 us
  starting transfers between devices: 6.19 us -> 0 us
  other arithmetic: 2.29 us -> 0 us
    pallas_call x1, Pallas kernels: 102 us -> 84.3 us  [track(): pl.pallas_call(functools.partial(track_kernel, strips, chain), out_shape=...]
    pallas_call x1, Pallas kernels: 23.9 us -> 12.7 us  [warp(): pl.pallas_call(warp_kernel, grid=(rows // BLOCK_ROWS,), out_shape=jax.Sha...]
    ppermute x2 -> x0, starting transfers between devices: 6.19 us -> none  [the longest x1 4.9 us: with_ends(): lax.ppermute(lax.slice_in_dim(array, length - 1, length, axis=dim), axis,...]
    convert_element_type x3 -> x0, other arithmetic: 2.18 us -> none  [the longest x1 1.45 us: local(): basis = spline_basis(0, columns, columns).astype(jnp.bfloat16)]
  transfers between devices with their start and end apart: 2 -> 0, of which waited for: 0 -> 0; matrix products, arithmetic and copies ran while one was open for 1% -> 0% of each run, Pallas kernels for 75% -> 0%
where the time goes in v2:
time: 98.6 us; the launch traced here: 98.3 us
  Pallas kernels  97.1 us (98%)
    pallas_call x1, Pallas kernels, track(): pl.pallas_call(functools.partial(track_kernel, strips, chain), out_shape=...  84.3 us
    pallas_call x1, Pallas kernels, warp(): pl.pallas_call(warp_kernel, grid=(rows // BLOCK_ROWS,), out_shape=jax.Sha...  12.7 us

profile of v2, /device:TPU:0, one launch (start us, length us, event | category | flops | bytes accessed | tf_op | source)
XLA Modules:
  0.0 98.3 jit_solution(12084183299186752050)
XLA Ops:
  0.6 84.3 %shard_map.50 = (f32[64,128]{1,0:T(8,128)}, bf16[512,128]{1,0:T(8,128)(2,1)}, f32[16,4096]{1,0:T(8,128)}) custom-call(bf16[512,4096]{1,0:T(8,128)(2,1)} %bitcast.3, bf16[512,4096]{1,0:T(8,128)(2,1)} %anchor_ref.1), custom_call_target="tpu_custom_call" | custom-call | tf_op jit(solution)/shard_map/pallas_call | solution.py:542
  85.0 0.0 copy-start
  85.0 12.7 %shard_map.51 = bf16[512,4096]{1,0:T(8,128)(2,1)} custom-call(bf16[512,4096]{1,0:T(8,128)(2,1)} %bitcast.4, bf16[512,4096]{1,0:T(8,128)(2,1)} %bitcast.5, bf16[512,4096]{1,0:T(8,128)(2,1)} %bitcast.6, f32[16,4096]{1,0:T(8,128)} %get-tuple-element.5.edges_ref, bf16[512,128]{1,0:T(8,128)(2,1)} %get-tuple-element.6.mixed_ref, ...), custom_call_target="tpu_custom_call" | custom-call | tf_op jit(solution)/shard_map/pallas_call | solution.py:84
  97.7 0.0 copy-done
  97.7 0.6 copy.6
Async XLA Ops:
  85.0 12.8 %copy-start = (f32[64,128]{1,0:T(8,128)S(1)}, f32[64,128]{1,0:T(8,128)}, u32[]{:S(2)}) copy-start(f32[64,128]{1,0:T(8,128)} %get-tuple-element.7) | copy-start | bytes 98308

commit v3 on v2

--- a/solution.py
+++ b/solution.py
@@ -12,7 +12,6 @@
 ITERATIONS = 4
 EPSILON = 1e-06
 SMOOTHING = 0.25
-EXACT = lax.Precision.HIGHEST
 BAND = 4
 SPLIT = 4
 LANES = 128
@@ -112,6 +111,10 @@
     return 16 + max(8, -(-knots // 8) * 8)
 
 
+def narrow_of(knots):
+    return -(-(knots + 8) // 8) * 8
+
+
 def base_of(strip, knots):
     return lax.div(strip * knots, 8) * 8
 
@@ -144,8 +147,6 @@
     rounded = lambda values: values.astype(BF16).astype(F32)
     single = rounded(spline_weight(place - knot.astype(F32)))
     product = single * rounded(spline_weight(place - (knot + band).astype(F32)))
-    large = rounded(product)
-    small = product - large
     one_lane = lax.broadcasted_iota(jnp.int32, (spacing, LANES), 1)
     one_knot = lax.rem(one_lane, GRID_SIZE)
 
@@ -162,9 +163,8 @@
             cols = slice(k * LANES, (k + 1) * LANES)
             reach = one_knot + (k * LANES // GRID_SIZE + lax.div(one_lane, GRID_SIZE))
             keep = close & (reach < GRID_SIZE)
-            for part, values in enumerate((large, small)):
-                rolled = jnp.where(keep, pltpu.roll(values[:, cols], shift, 1), 0.0)
-                pairs_ref[part, at, cols] = rolled.astype(BF16)
+            rolled = jnp.where(keep, pltpu.roll(product[:, cols], shift, 1), 0.0)
+            pairs_ref[at, cols] = rolled.astype(BF16)
 
 
 def fill_rows(wide, at, source, row, count, skip=0):
@@ -211,10 +211,10 @@
         for k in range(2):
             lin[1 + k] += dot(fields[2 * k], basis_ref[0, cut, :]) + dot(fields[2 * k + 1], basis_ref[1, cut, :])
         for k in range(3):
-            raw[k] += dot(fields[4 + k], pairs_ref[0, cut, :]) + dot(fields[4 + k], pairs_ref[1, cut, :])
-
-
-def rest_tables(wide, fixed, fixed_row, fields, basis_ref, lin, sums, rows, cols):
+            raw[k] += dot(fields[4 + k], pairs_ref[cut, :])
+
+
+def rest_tables(wide, fixed, fixed_row, fields, basis_ref, lin, sums, rows, cols, target=0):
     dot = functools.partial(jnp.dot, preferred_element_type=F32)
 
     @pl.loop(0, cols // SPAN)
@@ -235,7 +235,9 @@
         blocks(rows, start, body)
         cut = pl.ds(start, SPAN)
         here = pl.ds(0, rows)
-        lin[0, here] += dot(fields[0, here], basis_ref[0, cut, :]) + dot(fields[1, here], basis_ref[1, cut, :])
+        lin[0, pl.ds(target, rows)] += dot(fields[0, here], basis_ref[0, cut, :]) + dot(
+            fields[1, here], basis_ref[1, cut, :]
+        )
 
 
 def quad_tables(raw, quad):
@@ -252,20 +254,44 @@
     return jnp.concatenate(rows + [jnp.zeros((HEAD - 4, LANES), F32)], axis=0)
 
 
+def thirds(values):
+    high = values.astype(BF16).astype(F32)
+    rest = values - high
+    middle = rest.astype(BF16).astype(F32)
+    return high, middle, (rest - middle).astype(BF16).astype(F32)
+
+
+def mix(row_six, control):
+    high, middle, low = thirds(control)
+    six = jnp.concatenate([high, middle, high, low, middle, high], axis=0).astype(BF16)
+    return jnp.dot(row_six[...], six, preferred_element_type=F32)
+
+
+def project_rows(row_three, values):
+    window = row_three.shape[0] // 3
+    out = 0.0
+    for k, part in enumerate(thirds(values)):
+        product = jnp.dot(row_three[...], part.astype(BF16), preferred_element_type=F32)
+        for j in range(3 - k):
+            out += product[j * window : (j + 1) * window]
+    return out
+
+
 def grand(values):
     return jnp.sum(jnp.sum(values, axis=0, keepdims=True), axis=1, keepdims=True)
 
 
 def track_kernel(strips, chain, m_ref, anchor_ref, acc_ref, mixed_ref, edges_ref, *scratch):
-    (fixed, low, top, bottom, wide, fields, basis_ref, pairs_ref, lin, raw, quad, sums) = scratch[:12]
-    (row_basis, row_basis_t, moved, hist, parts, side, near, ends, grads) = scratch[12:21]
-    (quad_send, quad_recv, side_send, side_recv, near_send, near_recv) = scratch[21:27]
-    (end_send, end_recv, bulk_send, bulk_recv, local_sem) = scratch[27:]
+    (fixed, low, top, bottom, tail, first_row, last_row, wide, low_wide, fields, basis_ref, pairs_ref, lin, raw, quad, sums) = scratch[:16]
+    (row_six, row_three, moved, hist, parts, side, near, ends, grads) = scratch[16:25]
+    (quad_send, quad_recv, side_send, side_recv, near_send, near_recv) = scratch[25:31]
+    (end_send, end_recv, bulk_send, bulk_recv, local_sem) = scratch[31:]
     rows, cols = m_ref.shape
     half = rows // 2
     me, link = lax.axis_index("quad"), lax.axis_index("chain")
     knots = GRID_SIZE // strips
-    window = window_of(knots)
+    window, narrow = window_of(knots), narrow_of(knots)
+    early = ITERATIONS + 1
     spacing = rows * strips // GRID_SIZE
     pixel_count = float(rows * strips * cols)
     base = base_of(me, knots)
@@ -299,89 +325,87 @@
     def _():
         load_anchor.start()
 
-    @pl.when(me == 0)
-    def _():
-        top[...] = jnp.zeros_like(top)
-
-    @pl.when(me == strips - 1)
-    def _():
-        bottom[...] = jnp.zeros_like(bottom)
-        low[pl.ds(HALO + half, HALO), :] = jnp.zeros((HALO, cols), BF16)
-
-    @pl.when(first)
-    def _():
-        near[:, 0] = jnp.zeros_like(near[:, 0])
-        side[...] = jnp.zeros_like(side)
-
-    @pl.when(last)
-    def _():
-        near[:, 1] = jnp.zeros_like(near[:, 1])
-
+    first_row[...] = m_ref[pl.ds(0, HALO), :].astype(F32)[:1]
+    last_row[...] = m_ref[pl.ds(rows - HALO, HALO), :].astype(F32)[HALO - 1 :]
     begin = me * rows
-    row_basis[...] = strip_basis((rows, window), 0, begin, base - 8, spacing)
-    row_basis_t[...] = strip_basis((window, rows), 1, begin, base - 8, spacing)
-    for ref in (hist, grads, lin, raw, sums):
-        ref[...] = jnp.zeros_like(ref)
-    zeros = jnp.zeros((rows + 2 * EDGE, LANES), F32)
-    wide[:, pl.ds(0, LANES)] = zeros
-    wide[:, pl.ds(cols + LANES, LANES)] = zeros
-    column_tables(basis_ref, pairs_ref, cols // GRID_SIZE)
+    lane = lax.broadcasted_iota(jnp.int32, (rows, 6 * window), 1)
+    group = sum((lane >= k * window).astype(jnp.int32) for k in range(1, 6))
+    pixels = (begin + lax.broadcasted_iota(jnp.int32, (rows, 6 * window), 0)).astype(F32)
+    knot_pos = (base - 8 + lane - window * group).astype(F32)
+    high, middle, small = thirds(spline_weight((pixels + 0.5) * (1.0 / spacing) - knot_pos - 0.5))
+    is_middle = (group == 2) | (group == 4)
+    row_six[...] = jnp.where(group == 5, small, jnp.where(is_middle, middle, high)).astype(BF16)
+    rows_t = thirds(strip_basis((narrow, rows), 1, begin, me * knots - 4, spacing))
+    row_three[...] = jnp.concatenate(rows_t, axis=0).astype(BF16)
+    fill_body(wide, m_ref, 0, rows)
     cross = jnp.where(first, 0, strips - 1) + jnp.where(last, 0, strips - 1)
     pl.semaphore_wait(barrier, strips - 1 + chain - 1 + cross)
 
-    start_rows, end_rows = m_ref.at[pl.ds(0, HALO)], m_ref.at[pl.ds(rows - HALO, HALO)]
-    to_top = mesh_copy(end_rows, top, bulk_send.at[0], bulk_recv.at[0], {"quad": me + 1})
-    to_bottom = mesh_copy(start_rows, bottom, bulk_send.at[1], bulk_recv.at[1], {"quad": me - 1})
-    up = mesh_copy(
-        m_ref.at[pl.ds(0, half)], fixed.at[pl.ds(0, half)], bulk_send.at[2], bulk_recv.at[2], {"chain": link + 1}
-    )
-    down = mesh_copy(
-        m_ref.at[pl.ds(half - HALO, half + HALO)],
-        low.at[pl.ds(0, half + HALO)],
-        bulk_send.at[3],
-        bulk_recv.at[3],
-        {"chain": link - 1},
-    )
+    to_top = mesh_copy(last_row, top, bulk_send.at[0], bulk_recv.at[0], {"quad": me + 1})
+    to_bottom = mesh_copy(first_row, bottom, bulk_send.at[1], bulk_recv.at[1], {"quad": me - 1})
+    def up(count):
+        at = pl.ds(0, count)
+        return mesh_copy(m_ref.at[at], fixed.at[at], bulk_send.at[2], bulk_recv.at[2], {"chain": link + 1})
+
+    def down(count):
+        source = m_ref.at[pl.ds(rows - count - HALO, count + HALO)]
+        target = low.at[pl.ds(half - count, count + HALO)]
+        return mesh_copy(source, target, bulk_send.at[3], bulk_recv.at[3], {"chain": link - 1})
+
     across = mesh_copy(
-        start_rows,
-        low.at[pl.ds(HALO + half, HALO)],
+        first_row,
+        tail,
         bulk_send.at[4],
         bulk_recv.at[4],
         {"chain": link - 1, "quad": me - 1},
     )
     inner_top, inner_bottom = me > 0, me < strips - 1
     later, earlier = jnp.logical_not(last), jnp.logical_not(first)
+    even = lax.rem(link, 2) == 0
+    odd = jnp.logical_not(even)
+    wide_share = 3 * rows // 4
     pl.when(inner_bottom)(lambda: to_top.start())
     pl.when(inner_top)(lambda: to_bottom.start())
-    pl.when(later)(lambda: up.start())
-    pl.when(earlier)(lambda: down.start())
+    pl.when(later & even)(lambda: up(wide_share).start())
+    pl.when(later & odd)(lambda: up(half).start())
+    pl.when(earlier & odd)(lambda: down(rows - wide_share).start())
+    pl.when(earlier & even)(lambda: down(half).start())
     pl.when(jnp.logical_and(earlier, inner_top))(lambda: across.start())
 
-    fill_body(wide, m_ref, 0, rows)
+    @pl.when(me == 0)
+    def _():
+        top[...] = jnp.zeros_like(top)
+
+    @pl.when(me == strips - 1)
+    def _():
+        bottom[...] = jnp.zeros_like(bottom)
+        tail[...] = jnp.zeros_like(tail)
+
+    @pl.when(first)
+    def _():
+        near[:, 0] = jnp.zeros_like(near[:, 0])
+        side[...] = jnp.zeros_like(side)
+
+    @pl.when(last)
+    def _():
+        near[:, 1] = jnp.zeros_like(near[:, 1])
+
+    for ref in (hist, grads, lin, raw, sums):
+        ref[...] = jnp.zeros_like(ref)
+    zeros = jnp.zeros((rows + 2 * EDGE, LANES), F32)
+    for at in (0, cols + LANES):
+        wide[:, pl.ds(at, LANES)] = zeros
+        low_wide[:, pl.ds(at, LANES)] = zeros[: half + 2 * EDGE]
+    column_tables(basis_ref, pairs_ref, cols // GRID_SIZE)
     pl.when(inner_top)(lambda: to_top.wait_recv())
     pl.when(inner_bottom)(lambda: to_bottom.wait_recv())
-    for k, values in enumerate((top[...].astype(F32)[EDGE:], bottom[...].astype(F32)[:EDGE])):
+    for k, row in enumerate((top, bottom)):
+        values = jnp.broadcast_to(row[...], (EDGE, cols))
         edges_ref[pl.ds(k * EDGE, EDGE), :] = values
         wide[pl.ds(k * (EDGE + rows), EDGE), pl.ds(LANES, cols)] = values
 
     still_tables(wide, fields, basis_ref, pairs_ref, lin, raw, sums, rows, cols)
     quad_tables(raw, quad)
-
-    exact = functools.partial(jnp.dot, precision=EXACT, preferred_element_type=F32)
-
-    @pl.when(first)
-    def _():
-        load_anchor.wait()
-        rest_tables(wide, fixed, 0, fields, basis_ref, lin, sums, rows, cols)
-
-    @pl.when(earlier)
-    def _():
-        up.wait_recv()
-        rest_tables(wide, fixed, 0, fields, basis_ref, lin, sums, half, cols)
-
-    parts[0, me, pl.ds(0, HEAD)] = head_rows(sums, (0, 1, 2, 3))
-    for k in range(3):
-        parts[0, me, pl.ds(HEAD + k * window, window)] = 0.5 * exact(row_basis_t[...], lin[k])
 
     def spread(turn, count):
         copies = []
@@ -401,27 +425,44 @@
 
     def side_copy(row, step):
         to = {"chain": link + 1, "quad": lax.rem(me + step, strips)}
-        return mesh_copy(parts.at[ITERATIONS, me, pl.ds(0, HEAD + window)], side.at[row], side_send.at[step], side_recv.at[row], to)
-
-    sends = spread(0, HEAD + 3 * window)
-
-    @pl.when(later)
-    def _():
-        down.wait_recv()
+        return mesh_copy(parts.at[ITERATIONS, me, pl.ds(0, HEAD + narrow)], side.at[row], side_send.at[step], side_recv.at[row], to)
+
+    still_sums = (1, 3)
+
+    def own_part(wait, count):
+        wait()
+        sums[...] = jnp.zeros_like(sums)
+        rest_tables(wide, fixed, 0, fields, basis_ref, lin, sums, count, cols)
+        parts[0, me, pl.ds(HEAD, narrow)] = 0.5 * project_rows(row_three, lin[0])
+        parts[0, me, pl.ds(0, HEAD)] = head_rows(sums, (0, 2))
+
+    def later_part(count):
+        down(count).wait_recv()
         pl.when(inner_bottom)(lambda: across.wait_recv())
-        fill_body(wide, low, HALO, half)
-        fill_rows(wide, 0, low, 0, EDGE, EDGE)
-        tail = low[pl.ds(HALO + half, HALO), :].astype(F32)
-        wide[pl.ds(EDGE + half, EDGE), pl.ds(LANES, cols)] = tail[:EDGE]
+        fill_body(low_wide, low, HALO + half - count, count)
+        begin_low = half - count
+        fill_rows(low_wide, 0, low, begin_low, EDGE, EDGE)
+        low_wide[pl.ds(EDGE + count, EDGE), pl.ds(LANES, cols)] = jnp.broadcast_to(tail[...], (EDGE, cols))
         sums[...] = jnp.zeros_like(sums)
-        lin[0] = jnp.zeros_like(lin[0])
-        rest_tables(wide, m_ref, half, fields, basis_ref, lin, sums, half, cols)
+        lin[1] = jnp.zeros_like(lin[1])
+        rest_tables(low_wide, m_ref, rows - count, fields, basis_ref, lin.at[pl.ds(1, 1)], sums, count, cols, rows - count)
         parts[ITERATIONS, me, pl.ds(0, HEAD)] = head_rows(sums, (0, 2))
-        parts[ITERATIONS, me, pl.ds(HEAD, window)] = 0.5 * exact(row_basis_t[:, half:], lin[0, pl.ds(0, half)])
+        parts[ITERATIONS, me, pl.ds(HEAD, narrow)] = 0.5 * project_rows(row_three, lin[1])
         for step in range(strips):
             side_copy(me, step).start()
 
-    gathered(0, HEAD + 3 * window)
+    parts[early, me, pl.ds(0, HEAD)] = head_rows(sums, still_sums)
+    for k in range(2):
+        parts[early, me, pl.ds(HEAD + k * narrow, narrow)] = 0.5 * project_rows(row_three, lin[1 + k])
+    sends = spread(early, HEAD + 2 * narrow)
+    pl.when(even & later)(lambda: later_part(rows - wide_share))
+    pl.when(first)(lambda: own_part(load_anchor.wait, rows))
+    pl.when(even & earlier)(lambda: own_part(up(half).wait_recv, half))
+    pl.when(odd)(lambda: own_part(up(wide_share).wait_recv, wide_share))
+    sends += spread(0, HEAD + narrow)
+    pl.when(odd & later)(lambda: later_part(half))
+    gathered(early, HEAD + 2 * narrow)
+    gathered(0, HEAD + narrow)
 
     @pl.when(earlier)
     def _():
@@ -435,18 +476,19 @@
 
     def collect(ref, turn, offset, slot):
         for strip in range(strips):
-            at = strip * knots // 8 * 8
-            here = (strip, pl.ds(offset, window))
-            grads[slot, pl.ds(at, window)] += ref[here] if turn is None else ref[(turn, *here)]
+            here = (strip, pl.ds(offset, narrow))
+            grads[slot, pl.ds(strip * knots + 4, narrow)] += ref[here] if turn is None else ref[(turn, *here)]
         return grads[slot, pl.ds(8, GRID_SIZE)]
 
-    head = parts[0, 0, pl.ds(0, HEAD)] + side[0, pl.ds(0, HEAD)]
-    for strip in steps:
-        head = head + (parts[0, strip, pl.ds(0, HEAD)] + side[strip, pl.ds(0, HEAD)])
+    at = pl.ds(0, HEAD)
+    head = 0.0
+    for strip in range(strips):
+        head = head + (parts[0, strip, at] + parts[early, strip, at] + side[strip, at])
     head = jnp.sum(head, axis=1, keepdims=True)
     total = [head[k : k + 1, :] for k in range(4)]
     collect(side, None, HEAD, 0)
-    grad_rest, grad_still, grad_ones = (collect(parts, 0, HEAD + k * window, k) for k in range(3))
+    grad_rest = collect(parts, 0, HEAD, 0)
+    grad_still, grad_ones = (collect(parts, early, HEAD + k * narrow, 1 + k) for k in range(2))
     fixed_mean = total[0] / pixel_count
     block = 128
 
@@ -456,7 +498,7 @@
         before = hist[turn, pl.ds(8, GRID_SIZE)]
         smooth = 0.0
         if turn:
-            mixed_all = exact(row_basis[...], hist[turn, pl.ds(base, window)])
+            mixed_all = mix(row_six, hist[turn, pl.ds(base, window)])
             moved[...] = mixed_all.astype(BF16).astype(F32)
 
             @pl.loop(0, rows // block)
@@ -471,9 +513,9 @@
                     out += pltpu.roll(q * mixed + p * other, d, 1)
                 moved[r, :] = out
 
-            parts[turn, me, pl.ds(0, window)] = exact(row_basis_t[...], moved[...])
-            sends += spread(turn, window)
-            gathered(turn, window)
+            parts[turn, me, pl.ds(0, narrow)] = project_rows(row_three, moved[...])
+            sends += spread(turn, narrow)
+            gathered(turn, narrow)
             grad_extra = collect(parts, turn, 0, 2 + turn)
             moving_sum = moving_sum + grand(before * grad_ones)
             moving_sq = moving_sq + grand(before * (2.0 * grad_still + grad_extra))
@@ -512,7 +554,7 @@
         out = out + jnp.where(owner <= link, ends[owner], 0.0)
     acc_ref[...] = out
     hist[0, pl.ds(8, GRID_SIZE)] = out
-    mixed_ref[...] = exact(row_basis[...], hist[0, pl.ds(base, window)]).astype(BF16) * jnp.asarray(0.5, BF16)
+    mixed_ref[...] = mix(row_six, hist[0, pl.ds(base, window)]).astype(BF16) * jnp.asarray(0.5, BF16)
     for copy in sends:
         copy.wait_send()
     for turn in range(1, ITERATIONS):
@@ -522,12 +564,14 @@
         end_copy(link, step).wait_send()
     pl.when(inner_bottom)(lambda: to_top.wait_send())
     pl.when(inner_top)(lambda: to_bottom.wait_send())
-    pl.when(earlier)(lambda: down.wait_send())
+    pl.when(earlier & odd)(lambda: down(rows - wide_share).wait_send())
+    pl.when(earlier & even)(lambda: down(half).wait_send())
+    pl.when(later & even)(lambda: up(wide_share).wait_send())
+    pl.when(later & odd)(lambda: up(half).wait_send())
     pl.when(jnp.logical_and(earlier, inner_top))(lambda: across.wait_send())
 
     @pl.when(later)
     def _():
-        up.wait_send()
         for step in range(strips):
             side_copy(me, step).wait_send()
 
@@ -550,28 +594,30 @@
         out_specs=[vmem] * 3,
         scratch_shapes=[
             pltpu.VMEM((rows, cols), BF16),
-            pltpu.VMEM((rows // 2 + 2 * HALO, cols), BF16),
-            pltpu.VMEM((HALO, cols), BF16),
-            pltpu.VMEM((HALO, cols), BF16),
+            pltpu.VMEM((rows // 2 + HALO, cols), BF16),
+        ]
+        + [pltpu.VMEM((1, cols), F32)] * 5
+        + [
             pltpu.VMEM((rows + 2 * EDGE, cols + 2 * LANES), F32),
+            pltpu.VMEM((rows // 2 + 2 * EDGE, cols + 2 * LANES), F32),
             pltpu.VMEM((FIELDS, rows, SPAN), BF16),
             pltpu.VMEM((2, cols, LANES), BF16),
-            pltpu.VMEM((2, cols, BAND * GRID_SIZE), BF16),
+            pltpu.VMEM((cols, BAND * GRID_SIZE), BF16),
             pltpu.VMEM((3, rows, LANES), F32),
             pltpu.VMEM((3, rows, BAND * GRID_SIZE), F32),
             pltpu.VMEM((2 * BAND, rows, LANES), F32),
             pltpu.VMEM((4, 8, LANES), F32),
-            pltpu.VMEM((rows, window), F32),
-            pltpu.VMEM((window, rows), F32),
+            pltpu.VMEM((rows, 6 * window), BF16),
+            pltpu.VMEM((3 * narrow_of(GRID_SIZE // strips), rows), BF16),
             pltpu.VMEM((rows, LANES), F32),
             pltpu.VMEM((ITERATIONS + 1, tall, LANES), F32),
-            pltpu.VMEM((ITERATIONS + 1, strips, HEAD + 3 * window, LANES), F32),
-            pltpu.VMEM((strips, HEAD + window, LANES), F32),
+            pltpu.VMEM((ITERATIONS + 2, strips, HEAD + 2 * narrow_of(GRID_SIZE // strips), LANES), F32),
+            pltpu.VMEM((strips, HEAD + narrow_of(GRID_SIZE // strips), LANES), F32),
             pltpu.VMEM((ITERATIONS + 1, 2, GRID_SIZE, LANES), F32),
             pltpu.VMEM((chain, GRID_SIZE, LANES), F32),
             pltpu.VMEM((ITERATIONS + 2, tall, LANES), F32),
-            dma((ITERATIONS, strips)),
-            dma((ITERATIONS, strips)),
+            dma((ITERATIONS + 2, strips)),
+            dma((ITERATIONS + 2, strips)),
             dma((strips,)),
             dma((strips,)),
             dma((ITERATIONS + 1, 2)),

time: 98.6 us -> 90.2 us (0.915)
  Pallas kernels: 97.1 us -> 88.7 us
    pallas_call x1, Pallas kernels: 84.3 us -> 76 us  [track(): pl.pallas_call(functools.partial(track_kernel, strips, chain), out_shape=...]
where the time goes in v3:
time: 90.2 us; the launch traced here: 89.9 us
  Pallas kernels  88.7 us (98%)
    pallas_call x1, Pallas kernels, track(): pl.pallas_call(functools.partial(track_kernel, strips, chain), out_shape=...  76 us
    pallas_call x1, Pallas kernels, warp(): pl.pallas_call(warp_kernel, grid=(rows // BLOCK_ROWS,), out_shape=jax.Sha...  12.7 us

profile of v3, /device:TPU:0, one launch (start us, length us, event | category | flops | bytes accessed | tf_op | source)
XLA Modules:
  0.0 89.9 jit_solution(11359062179586394623)
XLA Ops:
  0.6 76.0 %shard_map.50 = (f32[64,128]{1,0:T(8,128)}, bf16[512,128]{1,0:T(8,128)(2,1)}, f32[16,4096]{1,0:T(8,128)}) custom-call(bf16[512,4096]{1,0:T(8,128)(2,1)} %bitcast.3, bf16[512,4096]{1,0:T(8,128)(2,1)} %anchor_ref.1), custom_call_target="tpu_custom_call" | custom-call | tf_op jit(solution)/shard_map/pallas_call | solution.py:586
  76.6 0.0 copy-start
  76.6 12.7 %shard_map.51 = bf16[512,4096]{1,0:T(8,128)(2,1)} custom-call(bf16[512,4096]{1,0:T(8,128)(2,1)} %bitcast.4, bf16[512,4096]{1,0:T(8,128)(2,1)} %bitcast.5, bf16[512,4096]{1,0:T(8,128)(2,1)} %bitcast.6, f32[16,4096]{1,0:T(8,128)} %get-tuple-element.5.edges_ref, bf16[512,128]{1,0:T(8,128)(2,1)} %get-tuple-element.6.mixed_ref, ...), custom_call_target="tpu_custom_call" | custom-call | tf_op jit(solution)/shard_map/pallas_call | solution.py:83
  89.3 0.0 copy-done
  89.3 0.6 copy.6
Async XLA Ops:
  76.6 12.7 %copy-start = (f32[64,128]{1,0:T(8,128)S(1)}, f32[64,128]{1,0:T(8,128)}, u32[]{:S(2)}) copy-start(f32[64,128]{1,0:T(8,128)} %get-tuple-element.7) | copy-start | bytes 98308

commit v4 on v3

--- a/solution.py
+++ b/solution.py
@@ -51,7 +51,8 @@
     return out
 
 
-def warp_kernel(above_ref, m_ref, below_ref, edges_ref, mixed_ref, flat_ref, out_ref, wide):
+def warp_kernel(above_ref, m_ref, below_ref, edges_ref, mixed_ref, flat_ref, acc_ref, out_ref, acc_out, wide):
+    acc_out[...] = acc_ref[...]
     step, rows, cols = pl.program_id(0), m_ref.shape[0], m_ref.shape[1]
     zeros = jnp.zeros((rows + 2 * EDGE, LANES), jnp.float32)
     wide[:, pl.ds(0, LANES)] = zeros
@@ -65,7 +66,7 @@
     )
     wide[pl.ds(EDGE, rows), inner] = m_ref[...].astype(jnp.float32)
 
-    @pl.loop(0, cols // BLOCK_COLS)
+    @pl.loop(0, cols // BLOCK_COLS, unroll=2)
     def _(j):
         c = pl.multiple_of(j * BLOCK_COLS, BLOCK_COLS)
         value, sx, sy = slopes_of(wide, 0, c)
@@ -75,7 +76,7 @@
         out_ref[:, pl.ds(c, BLOCK_COLS)] = (value + shift_x * sx + shift_y * sy).astype(jnp.bfloat16)
 
 
-def warp(moving, edges, mixed, flat):
+def warp(moving, edges, mixed, flat, accumulated):
     rows, cols = moving.shape
     thin = 2 * EDGE
     ratio, last = BLOCK_ROWS // thin, rows // thin - 1
@@ -83,7 +84,10 @@
     return pl.pallas_call(
         warp_kernel,
         grid=(rows // BLOCK_ROWS,),
-        out_shape=jax.ShapeDtypeStruct((rows, cols), jnp.bfloat16),
+        out_shape=(
+            jax.ShapeDtypeStruct((rows, cols), jnp.bfloat16),
+            jax.ShapeDtypeStruct(accumulated.shape, jnp.float32),
+        ),
         in_specs=[
             pl.BlockSpec((thin, cols), lambda i: (jnp.maximum(ratio * i - 1, 0), 0)),
             pl.BlockSpec((BLOCK_ROWS, cols), lambda i: (i, 0)),
@@ -91,11 +95,12 @@
             whole(edges.shape),
             pl.BlockSpec((BLOCK_ROWS, LANES), lambda i: (i, 0)),
             whole(flat.shape),
+            whole(accumulated.shape),
         ],
-        out_specs=pl.BlockSpec((BLOCK_ROWS, cols), lambda i: (i, 0)),
+        out_specs=(pl.BlockSpec((BLOCK_ROWS, cols), lambda i: (i, 0)), whole(accumulated.shape)),
         scratch_shapes=[pltpu.VMEM((BLOCK_ROWS + 2 * EDGE, cols + 2 * LANES), jnp.float32)],
         compiler_params=pltpu.CompilerParams(vmem_limit_bytes=VMEM_BYTES),
-    )(moving, moving, moving, edges, mixed, flat)
+    )(moving, moving, moving, edges, mixed, flat, accumulated)
 
 
 MESH = pl.DeviceIdType.MESH
@@ -637,7 +642,7 @@
 def local(sections, anchor):
     moving = sections[0]
     accumulated, mixed, edges = track(moving, anchor)
-    registered = warp(moving, edges, mixed, flat_table(moving.shape[1]))
+    registered, accumulated = warp(moving, edges, mixed, flat_table(moving.shape[1]), accumulated)
     return registered[None], accumulated[None]
 
 

time: 90.2 us -> 89.1 us (0.988)
  no operation moved by 1% of the time
where the time goes in v4:
time: 89.1 us; the launch traced here: 88.7 us
  Pallas kernels  88.1 us (99%)
    pallas_call x1, Pallas kernels, track(): pl.pallas_call(functools.partial(track_kernel, strips, chain), out_shape=...  76 us
    pallas_call x1, Pallas kernels, warp(): pl.pallas_call(warp_kernel, grid=(rows // BLOCK_ROWS,), out_shape=(jax.Sh...  12.1 us

profile of v4, /device:TPU:0, one launch (start us, length us, event | category | flops | bytes accessed | tf_op | source)
XLA Modules:
  0.0 88.7 jit_solution(9106493478691639935)
XLA Ops:
  0.6 76.0 %shard_map.50 = (f32[64,128]{1,0:T(8,128)}, bf16[512,128]{1,0:T(8,128)(2,1)}, f32[16,4096]{1,0:T(8,128)}) custom-call(bf16[512,4096]{1,0:T(8,128)(2,1)} %bitcast.3, bf16[512,4096]{1,0:T(8,128)(2,1)} %anchor_ref.1), custom_call_target="tpu_custom_call" | custom-call | tf_op jit(solution)/shard_map/pallas_call | solution.py:591
  76.6 12.1 %shard_map.51 = (bf16[512,4096]{1,0:T(8,128)(2,1)}, f32[64,128]{1,0:T(8,128)}) custom-call(bf16[512,4096]{1,0:T(8,128)(2,1)} %bitcast.4, bf16[512,4096]{1,0:T(8,128)(2,1)} %bitcast.5, bf16[512,4096]{1,0:T(8,128)(2,1)} %bitcast.6, f32[16,4096]{1,0:T(8,128)} %get-tuple-element.7.edges_ref, bf16[512,128]{1,0:T(8,128)(2,1)} %get-tuple-element.8.mixed_ref, ...), custom_call_target="tpu_custom_call" | custom-call | tf_op jit(solution)/shard_map/pallas_call | solution.py:84
